TPU v7x, 128 devices: a whole 4x4x4 slice. The times are simulated.
128 devices in a mesh: seq: 8 (over x, core), span: 16 (over y, z).
Axes of the slice: x: 4, y: 4, z: 4, core: 2. Of those that a mesh axis runs over, the one named last changes fastest.
Arguments:
- llm_input: bfloat16 [1024, 5120], P(('seq', 'span')), may hold values from -6 to 6
- hidden_grad: bfloat16 [1024, 32768], P(None, ('seq', 'span')), may hold values from -1.5 to 1.5
- gate_act: bfloat16 [1024, 32768], P(None, ('seq', 'span')), may hold values from -6 to 6
- up_weight: bfloat16 [5120, 32768], P(None, ('seq', 'span')), may hold values from -0.078125 to 0.078125
- span_counts: int32 [32], replicated, may hold values from 16 to 48, as said below
- row_ticks: int32 [1024], replicated, may hold values from 0 to 47, as said below
- encoder_out: bfloat16 [16, 384, 1280], P('span'), may hold values from -6 to 6
- mlp_input: bfloat16 [16, 384, 1280], P('span'), may hold values from -6 to 6
- post_gain: float32 [1280], replicated, may hold values from 0.5 to 1.5
- post_bias: float32 [1280], replicated, may hold values from -3 to 3
- adapter_in: bfloat16 [5120, 5120], P(None, 'seq'), may hold values from -0.078125 to 0.078125
- adapter_out: bfloat16 [5120, 5120], P('seq'), may hold values from -0.078125 to 0.078125
- expand_weight: bfloat16 [1280, 5120], P(None, 'seq'), may hold values from -0.15625 to 0.15625
- expand_bias: float32 [5120], P('seq'), may hold values from -3 to 3
- contract_weight: bfloat16 [5120, 1280], P('seq'), may hold values from -0.078125 to 0.078125
Outputs:
- gate_act_grad: bfloat16 [1024, 32768], P(None, ('seq', 'span'))
- up_weight_grad: bfloat16 [5120, 32768], P(None, ('seq', 'span'))
- adapter_in_grad: bfloat16 [5120, 5120], P('span', 'seq')
- adapter_out_grad: bfloat16 [5120, 5120], P(('seq', 'span'))
- expand_weight_grad: bfloat16 [1280, 5120], P('span', 'seq')
- contract_weight_grad: bfloat16 [5120, 1280], P(('seq', 'span'))
- expand_bias_grad: float32 [5120], P('seq')
- post_gain_grad: float32 [1280], replicated
- post_bias_grad: float32 [1280], replicated
- contract_bias_grad: float32 [1280], replicated
- encoder_out_grad: bfloat16 [16, 384, 1280], P('span', 'seq')
- mlp_input_grad: bfloat16 [16, 384, 1280], P('span', 'seq')
Inputs may be any that keep to these rules, and one draw needn't show every extreme that they name: span_counts sums to 1024; its largest entry is exactly 48. `row_ticks`: the rows of each span are consecutive in the sequence, spans in order of their number, span k holding span_counts[k] rows; inside a span the tick rises by one from row to row.
All inputs are finite; a program needn't handle non-finite values.
Results may differ from a plain program's by a relative error of at most 0.03.
Values may be sent and summed in bfloat16 or wider, within the bound.
No kernel may reach another device: no remote copies, remote signals or barrier semaphores. Data moves between devices by JAX's collectives and lax.ppermute only.
A program may use at most 192 MiB of HBM per device.

v0:
```python
import math

import jax
import jax.numpy as jnp
from jax import lax
from jax.experimental import pallas as pl
from jax.sharding import PartitionSpec as P


STACK = 4
CH_DEV = 2


EPSILON = 1e-05


def exchanged(pieces, axis):
    return lax.all_to_all(pieces, axis, 0, 0, tiled=True)


def sent_and_summed(shard, axis):
    size = lax.axis_size(axis)
    pieces = exchanged(shard.reshape(size, shard.shape[0] // size, *shard.shape[1:]), axis)
    return jnp.sum(pieces.astype(jnp.float32), axis=0)


def permuted_sum(pieces, axis):
    size = lax.axis_size(axis)
    index = lax.axis_index(axis)
    mine = lax.dynamic_index_in_dim(pieces, index, 0, keepdims=False)
    arrived = []
    for step in range(1, size):
        piece = lax.dynamic_index_in_dim(pieces, (index + step) % size, 0, keepdims=False)
        arrived.append(lax.ppermute(piece, axis, [(i, (i + step) % size) for i in range(size)]))
    total = mine.astype(jnp.float32)
    for piece in arrived:
        total = total + piece.astype(jnp.float32)
    return total


def blocks_swapped(array, outer, inner):
    blocks = array.reshape(outer, inner, -1, array.shape[1])
    return jnp.swapaxes(blocks, 0, 1).reshape(array.shape)


def gelu_value(values):
    return 0.5 * values * (1.0 + lax.erf(values * (1.0 / math.sqrt(2.0))))


def gelu_slope(values):
    cumulative = 0.5 * (1.0 + lax.erf(values * (1.0 / math.sqrt(2.0))))
    return cumulative + values * jnp.exp(-0.5 * values * values) * (1.0 / math.sqrt(2.0 * math.pi))


def locate_rows(span_counts, row_ticks, capacity):
    span_ends = jnp.cumsum(span_counts)
    positions = jnp.arange(row_ticks.shape[0], dtype=jnp.int32)
    span_of = jnp.sum((positions[:, None] >= span_ends[None, :]).astype(jnp.int32), axis=1)
    return span_of * capacity + row_ticks


def contract_last(left, right):
    return lax.dot_general(
        left, right, (((1,), (1,)), ((), ())), preferred_element_type=jnp.float32
    )


def contract_first(left, right):
    return lax.dot_general(
        left, right, (((0,), (0,)), ((), ())), preferred_element_type=jnp.float32
    )


def column_block_kernel(hidden_ref, gate_ref, weight_ref, grad_ref, out_ref):
    @pl.when(pl.program_id(0) == 0)
    def _():
        product = hidden_ref[...].astype(jnp.float32) * gate_ref[...].astype(jnp.float32)
        grad_ref[...] = product.astype(grad_ref.dtype)

    out_ref[0] = contract_last(grad_ref[...], weight_ref[...]).astype(out_ref.dtype)


def column_blocks(hidden_grad, gate_act, weight, blocks):
    rows, inner = hidden_grad.shape
    width = weight.shape[0] // blocks
    whole = pl.BlockSpec((rows, inner), lambda i: (0, 0))
    return pl.pallas_call(
        column_block_kernel,
        grid=(blocks,),
        in_specs=[whole, whole, pl.BlockSpec((width, inner), lambda i: (i, 0))],
        out_specs=[whole, pl.BlockSpec((1, rows, width), lambda i: (i, 0, 0))],
        out_shape=[
            jax.ShapeDtypeStruct((rows, inner), jnp.bfloat16),
            jax.ShapeDtypeStruct((blocks, rows, width), jnp.bfloat16),
        ],
        cost_estimate=pl.CostEstimate(
            flops=2 * rows * inner * width * blocks,
            bytes_accessed=2 * (3 * rows * inner + blocks * width * (inner + rows)),
            transcendentals=0,
        ),
        name="column_blocks",
    )(hidden_grad, gate_act, weight)


def normalized(frames):
    centre = frames - jnp.mean(frames, axis=1, keepdims=True)
    rstd = lax.rsqrt(jnp.mean(centre * centre, axis=1, keepdims=True) + EPSILON)
    return centre * rstd, rstd


def step(
    llm_input,
    hidden_grad,
    gate_act,
    up_weight,
    span_counts,
    row_ticks,
    encoder_out,
    mlp_input,
    post_gain,
    post_bias,
    adapter_in,
    adapter_out,
    expand_weight,
    expand_bias,
    contract_weight,
):
    rows_all = row_ticks.shape[0]
    seq_size = lax.axis_size("seq")
    owner_count = lax.axis_size("span")
    seq_index = lax.axis_index("seq")
    frames_each = encoder_out.shape[1]
    width = encoder_out.shape[2]
    slots_each = frames_each // STACK
    capacity = slots_each // CH_DEV
    total_slots = owner_count * slots_each
    mine_frames = frames_each // seq_size

    piece = lax.all_gather(llm_input, "seq", axis=0, tiled=True)
    piece = lax.all_gather(piece, "span", axis=0, tiled=True)
    up_grad, blocks = column_blocks(hidden_grad, gate_act, up_weight, seq_size)
    partial_rows = lax.psum_scatter(
        blocks.reshape(seq_size * rows_all, blocks.shape[2]),
        "seq",
        scatter_dimension=0,
        tiled=True,
    )

    hidden_rows = blocks_swapped(hidden_grad, seq_size, owner_count)
    up_grad_rows = blocks_swapped(up_grad, seq_size, owner_count)

    slot_of = locate_rows(span_counts, row_ticks, capacity)
    matches = jnp.arange(total_slots, dtype=jnp.int32)[:, None] == slot_of[None, :]
    placing = matches.astype(jnp.bfloat16)
    nhat, rstd = normalized(encoder_out[0].astype(jnp.float32))
    stacked = (nhat * post_gain + post_bias).reshape(slots_each, STACK * width).astype(jnp.bfloat16)
    pre_act = jnp.dot(stacked, adapter_in, preferred_element_type=jnp.float32)
    activity = gelu_value(pre_act).astype(jnp.bfloat16)
    act_slope = gelu_slope(pre_act)
    activity_all = lax.all_gather(activity, "span", axis=0, tiled=True)
    columns = exchanged(
        jnp.moveaxis(stacked.reshape(slots_each, owner_count, -1), 1, 0), "span"
    ).reshape(total_slots, -1)
    inputs = mlp_input[0]
    hidden_pre = jnp.dot(inputs, expand_weight, preferred_element_type=jnp.float32) + expand_bias
    hidden_act = gelu_value(hidden_pre).astype(jnp.bfloat16)
    hidden_slope = gelu_slope(hidden_pre)
    (
        partial_rows,
        placing,
        act_slope,
        columns,
        hidden_act,
        hidden_slope,
        nhat,
        rstd,
        hidden_rows,
        up_grad_rows,
    ) = lax.optimization_barrier(
        (
            partial_rows,
            placing,
            act_slope,
            columns,
            hidden_act,
            hidden_slope,
            nhat,
            rstd,
            hidden_rows,
            up_grad_rows,
        )
    )

    partial_slots = jnp.dot(placing, partial_rows, preferred_element_type=jnp.float32)
    token_block = sent_and_summed(partial_slots.astype(jnp.bfloat16), "span").astype(jnp.bfloat16)
    token_grad = lax.all_gather(token_block, "seq", axis=1, tiled=True)

    pre_grad = (contract_last(token_grad, adapter_out) * act_slope).astype(jnp.bfloat16)
    normed_part = contract_last(pre_grad, adapter_in).astype(jnp.bfloat16)
    pre_grad_all = lax.all_gather(pre_grad, "span", axis=0, tiled=True)
    normed_part, token_grad, piece = lax.optimization_barrier((normed_part, token_grad, piece))
    normed_pieces = exchanged(normed_part.reshape(seq_size, mine_frames, width), "seq")

    token_cols = jnp.moveaxis(token_grad.reshape(slots_each, owner_count, -1), 1, 0)

    up_rows = jnp.dot(piece, up_weight, preferred_element_type=jnp.float32)
    gate_rows = (hidden_rows.astype(jnp.float32) * up_rows).astype(jnp.bfloat16)
    gate_act_grad = blocks_swapped(gate_rows, owner_count, seq_size)
    up_weight_grad = contract_first(piece, up_grad_rows).astype(jnp.bfloat16)
    normed_pieces, gate_act_grad, up_weight_grad, token_cols = lax.optimization_barrier(
        (normed_pieces, gate_act_grad, up_weight_grad, token_cols)
    )
    token_cols = exchanged(token_cols, "span").reshape(total_slots, -1)

    normed_mine = jnp.sum(normed_pieces.astype(jnp.float32), axis=0).astype(jnp.bfloat16)
    normed_grad = lax.all_gather(normed_mine, "seq", axis=0, tiled=True)
    scaled = normed_grad.astype(jnp.float32) * post_gain
    resid = rstd * (
        scaled
        - jnp.mean(scaled, axis=1, keepdims=True)
        - nhat * jnp.mean(scaled * nhat, axis=1, keepdims=True)
    )
    resid = resid.astype(jnp.bfloat16)

    contract_part = contract_first(hidden_act, resid).astype(jnp.bfloat16)
    contract_part, resid, token_cols = lax.optimization_barrier((contract_part, resid, token_cols))
    contract_pieces = exchanged(contract_part.reshape(owner_count, -1, width), "span")
    hidden_pre_grad = (contract_last(resid, contract_weight) * hidden_slope).astype(jnp.bfloat16)
    expand_part = contract_first(inputs, hidden_pre_grad).astype(jnp.bfloat16)
    expand_part, hidden_pre_grad, activity_all = lax.optimization_barrier(
        (expand_part, hidden_pre_grad, activity_all)
    )
    mlp_part = contract_last(hidden_pre_grad, expand_weight).astype(jnp.bfloat16)
    out_part = contract_first(activity_all, token_cols).astype(jnp.bfloat16)
    mlp_part, hidden_pre_grad, columns, normed_grad = lax.optimization_barrier(
        (mlp_part, hidden_pre_grad, columns, normed_grad)
    )
    rows = expand_part.shape[0] // owner_count
    packed = jnp.concatenate(
        [
            expand_part.reshape(owner_count, rows, -1),
            out_part.reshape(owner_count, -1, expand_part.shape[1]),
        ],
        axis=1,
    )
    packed, contract_pieces = lax.optimization_barrier((packed, contract_pieces))
    packed = exchanged(packed, "span")
    contract_weight_grad = jnp.sum(contract_pieces.astype(jnp.float32), axis=0).astype(jnp.bfloat16)
    mlp_input_grad = permuted_sum(
        mlp_part.reshape(seq_size, mine_frames, width), "seq"
    ).astype(jnp.bfloat16)

    adapter_in_grad = contract_first(columns, pre_grad_all).astype(jnp.bfloat16)

    normed_grad = normed_grad.astype(jnp.float32)
    sums = jnp.concatenate(
        [
            jnp.sum(normed_grad * nhat, axis=0),
            jnp.sum(normed_grad, axis=0),
            jnp.sum(resid.astype(jnp.float32), axis=0),
            jnp.sum(hidden_pre_grad.astype(jnp.float32), axis=0),
        ]
    )
    sums = jnp.sum(lax.all_gather(sums, "span", axis=0), axis=0)
    post_gain_grad, post_bias_grad, contract_bias_grad, expand_bias_grad = (
        sums[:width],
        sums[width : 2 * width],
        sums[2 * width : 3 * width],
        sums[3 * width :],
    )
    expand_weight_grad = jnp.sum(packed[:, :rows].astype(jnp.float32), axis=0).astype(jnp.bfloat16)
    out_rows = packed[:, rows:].reshape(owner_count, -1, out_part.shape[1])
    adapter_out_grad = jnp.moveaxis(out_rows, 0, 1).reshape(out_rows.shape[1], -1)
    resid_mine = lax.dynamic_slice_in_dim(resid, seq_index * mine_frames, mine_frames, 0)
    return (
        gate_act_grad,
        up_weight_grad,
        adapter_in_grad,
        adapter_out_grad,
        expand_weight_grad,
        contract_weight_grad,
        expand_bias_grad,
        post_gain_grad,
        post_bias_grad,
        contract_bias_grad,
        resid_mine.reshape(1, mine_frames, width),
        mlp_input_grad.reshape(1, mine_frames, width),
    )


def solution(mesh):
    return jax.shard_map(
        step,
        mesh=mesh,
        in_specs=(
            P(("seq", "span"), None),
            P(None, ("seq", "span")),
            P(None, ("seq", "span")),
            P(None, ("seq", "span")),
            P(),
            P(),
            P("span", None, None),
            P("span", None, None),
            P(),
            P(),
            P(None, "seq"),
            P("seq", None),
            P(None, "seq"),
            P("seq"),
            P("seq", None),
        ),
        out_specs=(
            P(None, ("seq", "span")),
            P(None, ("seq", "span")),
            P("span", "seq"),
            P(("seq", "span"), None),
            P("span", "seq"),
            P(("seq", "span"), None),
            P("seq"),
            P(),
            P(),
            P(),
            P("span", "seq", None),
            P("span", "seq", None),
        ),
        check_vma=False,
    )
```

profile of v0, /device:TPU:1, one launch (start us, length us, event | category | flops | bytes accessed | tf_op | source)
XLA Modules:
  0.0 361.2 jit_solution(8413076038001563795)
XLA Ops:
  8.1 9.8 %column_blocks.1 = (bf16[1024,256]{1,0:T(8,128)(2,1)}, bf16[8,1024,640]{2,1,0:T(8,128)(2,1)}) custom-call(bf16[1024,256]{1,0:T(8,128)(2,1)} %hidden_ref.1, bf16[1024,256]{1,0:T(8,128)(2,1)} %gate_ref.1, bf16[5120,256]{1,0:T(8,128)(2,1)} %weight_ref.1), custom_call_target="tpu_custom_call" | custom-call | flops 2684354560 | bytes 14680064 | tf_op jit(solution)/shard_map/column_blocks/pallas_call | solution.py:87
  18.8 16.0 %all_gather.25 = bf16[64,5120]{1,0:T(8,128)(2,1)} all-gather(bf16[8,5120]{1,0:T(8,128)(2,1)S(1)} %copy-done.20), channel_id=1, replica_groups=mesh['seq'=8,'span'=16] {'seq'}, dimensions={0}, use_global_device_ids=true | all-gather | bytes 737280 | tf_op jit(solution)/shard_map/all_gather | solution.py:139
  34.8 2.2 reshape.214
  38.3 3.9 %fusion.11 = bf16[16,96,320]{2,1,0:T(8,128)(2,1)} fusion(f32[96,16,320]{2,1,0:T(8,128)} %reshape.214, f32[16,320]{1,0:T(8,128)S(1)} %add.172, f32[16,320]{1,0:T(8,128)S(1)} %mul.187, f32[96,16]{0,1:T(8,128)S(1)} %bitcast.109, f32[96,16]{0,1:T(8,128)S(1)} %bitcast.110), kind=kLoop, calls=%fused_computation.37 | loop fusion | flops 2457600 | bytes 3002368 | tf_op jit(solution)/shard_map/transpose | solution.py:162
  42.2 8.4 %all-to-all-start = ((bf16[16,96,320]{2,1,0:T(8,128)(2,1)}), bf16[16,96,320]{2,1,0:T(8,128)(2,1)}, u32[]{:S(2)}, u32[]{:S(2)}) async-start(bf16[16,96,320]{2,1,0:T(8,128)(2,1)} %fusion.11), calls=%async_computation.1 | async-start | bytes 2359296 | tf_op jit(solution)/shard_map/all_to_all | solution.py:18
  50.7 1.8 reshape.213
  56.5 1.9 copy.66
  59.7 3.2 fusion
  64.6 2.2 fusion.16
  68.1 2.1 multiply_convert_fusion.2
  70.3 6.3 %all-to-all-done = bf16[16,96,320]{2,1,0:T(8,128)(2,1)} async-done(((bf16[16,96,320]{2,1,0:T(8,128)(2,1)}), bf16[16,96,320]{2,1,0:T(8,128)(2,1)}, u32[]{:S(2)}, u32[]{:S(2)}) %all-to-all-start) | async-done | bytes 983072 | tf_op jit(solution)/shard_map/all_to_all | solution.py:18
  76.6 6.5 %reduce-scatter.2.cloned.1.call-done = bf16[1024,640]{1,0:T(8,128)(2,1)} async-done(((bf16[8192,640]{1,0:T(8,128)(2,1)}), bf16[1024,640]{1,0:T(8,128)(2,1)}) %reduce-scatter.2.cloned.1.call-update) | async-done | bytes 1310736 | tf_op jit(solution)/shard_map/reduce_scatter | solution.py:142
  83.2 6.4 %convolution_convert_fusion.2 = bf16[1536,640]{1,0:T(8,128)(2,1)} fusion(bf16[1536,1024]{1,0:T(8,128)(2,1)} %fusion, bf16[1024,640]{1,0:T(8,128)(2,1)} %reduce-scatter.2.cloned.1.call-done), kind=kOutput, calls=%fused_computation.4 | convolution fusion | flops 2014248960 | bytes 6422528 | tf_op jit(solution)/shard_map/dot_general | solution.py:194
  89.6 7.1 %all-to-all-start.1 = ((bf16[16,96,640]{2,1,0:T(8,128)(2,1)}), bf16[16,96,640]{2,1,0:T(8,128)(2,1)}, u32[]{:S(2)}, u32[]{:S(2)}) async-start(bf16[16,96,640]{2,1,0:T(8,128)(2,1)} %bitcast.99), calls=%async_computation.2 | async-start | bytes 3932160 | tf_op jit(solution)/shard_map/all_to_all | solution.py:18
  97.4 41.8 %all-to-all-done.1 = bf16[16,96,640]{2,1,0:T(8,128)(2,1)} async-done(((bf16[16,96,640]{2,1,0:T(8,128)(2,1)}), bf16[16,96,640]{2,1,0:T(8,128)(2,1)}, u32[]{:S(2)}, u32[]{:S(2)}) %all-to-all-start.1) | async-done | bytes 1966112 | tf_op jit(solution)/shard_map/all_to_all | solution.py:18
  139.1 1.8 reduce_sum.141
  141.0 16.0 %all_gather.24 = bf16[96,5120]{1,0:T(8,128)(2,1)S(1)} all-gather(bf16[96,640]{1,0:T(8,128)(2,1)S(1)} %reduce_sum.141), channel_id=1, replica_groups=mesh['seq'=8,'span'=16] {'seq'}, dimensions={1}, use_global_device_ids=true | all-gather | bytes 1105920 | tf_op jit(solution)/shard_map/all_gather | solution.py:196
  157.0 4.9 %fusion.12 = bf16[96,640]{1,0:T(8,128)(2,1)S(1)} fusion(f32[96,640]{1,0:T(8,128)S(1)} %get-tuple-element.47, bf16[96,5120]{1,0:T(8,128)(2,1)S(1)} %all_gather.24, bf16[640,5120]{1,0:T(8,128)(2,1)} %param.26), kind=kOutput, calls=%fused_computation.39 | convolution fusion | flops 629268480 | bytes 7905280 | tf_op jit(solution)/shard_map/dot_general | solution.py:63
  162.0 6.0 %convolution_convert_fusion.1 = bf16[96,5120]{1,0:T(8,128)(2,1)} fusion(bf16[96,640]{1,0:T(8,128)(2,1)S(1)} %fusion.12, bf16[5120,640]{1,0:T(8,128)(2,1)} %param.25), kind=kOutput, calls=%fused_computation.3 | convolution fusion | flops 629637120 | bytes 7659520 | tf_op jit(solution)/shard_map/dot_general | solution.py:63
  167.9 7.7 %fusion.9 = bf16[1024,256]{1,0:T(8,128)(2,1)S(1)} fusion(bf16[1024,5120]{1,0:T(8,128)(2,1)} %all-gather.6.cloned.1.call-done, bf16[5120,256]{1,0:T(8,128)(2,1)} %weight_ref.1, bf16[1024,256]{1,0:T(8,128)(2,1)} %bitcast.105), kind=kOutput, calls=%fused_computation.33 | convolution fusion | flops 2685140992 | bytes 14155776 | tf_op jit(solution)/shard_map/dot_general | solution.py:206
  178.3 2.5 reshape.200
  180.8 3.6 %all-to-all-start.2 = ((bf16[8,48,1280]{2,1,0:T(8,128)(2,1)}), bf16[8,48,1280]{2,1,0:T(8,128)(2,1)S(1)}, u32[]{:S(2)}, u32[]{:S(2)}) async-start(bf16[8,48,1280]{2,1,0:T(8,128)(2,1)} %reshape.200), calls=%async_computation.3 | async-start | bytes 1966080 | tf_op jit(solution)/shard_map/all_to_all | solution.py:18
  185.0 8.7 %convolution_convert_fusion = bf16[5120,256]{1,0:T(8,128)(2,1)} fusion(bf16[1024,5120]{1,0:T(8,128)(2,1)} %all-gather.6.cloned.1.call-done, bf16[1024,256]{1,0:T(8,128)(2,1)S(1)} %bitcast.104), kind=kOutput, calls=%fused_computation | convolution fusion | flops 2685665280 | bytes 13631488 | tf_op jit(solution)/shard_map/dot_general | solution.py:69
  193.7 5.1 %all-to-all-done.2 = bf16[8,48,1280]{2,1,0:T(8,128)(2,1)S(1)} async-done(((bf16[8,48,1280]{2,1,0:T(8,128)(2,1)}), bf16[8,48,1280]{2,1,0:T(8,128)(2,1)S(1)}, u32[]{:S(2)}, u32[]{:S(2)}) %all-to-all-start.2) | async-done | bytes 983072 | tf_op jit(solution)/shard_map/all_to_all | solution.py:18
  198.9 14.5 %all_gather.27 = bf16[384,1280]{1,0:T(8,128)(2,1)S(1)} all-gather(bf16[48,1280]{1,0:T(8,128)(2,1)S(1)} %reduce_sum.142), channel_id=1, replica_groups=mesh['seq'=8,'span'=16] {'seq'}, dimensions={0}, use_global_device_ids=true | all-gather | bytes 1105920 | tf_op jit(solution)/shard_map/all_gather | solution.py:216
  213.4 2.6 copy.68
  216.0 9.5 %all-to-all-start.3 = ((bf16[16,96,320]{2,1,0:T(8,128)(2,1)}), bf16[16,96,320]{2,1,0:T(8,128)(2,1)}, u32[]{:S(2)}, u32[]{:S(2)}) async-start(bf16[16,96,320]{2,1,0:T(8,128)(2,1)} %copy.68), calls=%async_computation.4 | async-start | bytes 2359296 | tf_op jit(solution)/shard_map/all_to_all | solution.py:18
  225.5 2.1 fusion.7
  229.2 2.2 convolution_convert_fusion.4
  231.4 15.2 %all-to-all-done.3 = bf16[16,96,320]{2,1,0:T(8,128)(2,1)} async-done(((bf16[16,96,320]{2,1,0:T(8,128)(2,1)}), bf16[16,96,320]{2,1,0:T(8,128)(2,1)}, u32[]{:S(2)}, u32[]{:S(2)}) %all-to-all-start.3) | async-done | bytes 983072 | tf_op jit(solution)/shard_map/all_to_all | solution.py:18
  246.6 5.9 %all-to-all-start.4 = ((bf16[16,40,1280]{2,1,0:T(8,128)(2,1)}), bf16[16,40,1280]{2,1,0:T(8,128)(2,1)}, u32[]{:S(2)}, u32[]{:S(2)}) async-start(bf16[16,40,1280]{2,1,0:T(8,128)(2,1)} %bitcast.96), calls=%async_computation.5 | async-start | bytes 3276800 | tf_op jit(solution)/shard_map/all_to_all | solution.py:18
  252.5 3.0 fusion.10
  255.6 2.3 fusion.1
  259.8 1.8 collective-permute-start
  264.3 2.0 collective-permute-start.3
  266.3 2.6 collective-permute-start.4
  268.9 2.3 convolution_convert_fusion.6
  272.7 3.6 copy.69
  276.3 3.0 pad_maximum_fusion
  279.3 7.1 %all-to-all-start.5 = ((bf16[16,100,640]{2,1,0:T(8,128)(2,1)}), bf16[16,100,640]{2,1,0:T(8,128)(2,1)}, u32[]{:S(2)}, u32[]{:S(2)}) async-start(bf16[16,100,640]{2,1,0:T(8,128)(2,1)} %pad_maximum_fusion), calls=%async_computation.6 | async-start | bytes 4259840 | tf_op jit(solution)/shard_map/all_to_all | solution.py:18
  287.8 1.9 fusion.6
  289.8 39.4 %all-gather.1 = f32[16,1,4480]{2,1,0:T(1,128)S(1)} all-gather(f32[1,1,4480]{2,1,0:T(1,128)S(1)} %reshape.217), channel_id=2, replica_groups=mesh['seq'=8,'span'=16] {'span'}, dimensions={0}, use_global_device_ids=true | all-gather | bytes 304640 | tf_op jit(solution)/shard_map/all_gather | solution.py:264
  331.8 3.3 collective-permute-start.6
  335.7 4.8 %collective-permute-done.6 = bf16[48,1280]{1,0:T(8,128)(2,1)S(1)} collective-permute-done((bf16[48,1280]{1,0:T(8,128)(2,1)S(1)}, bf16[48,1280]{1,0:T(8,128)(2,1)S(1)}, u32[]{:S(2)}, u32[]{:S(2)}) %collective-permute-start.6) | collective-permute-done | bytes 122912 | tf_op jit(solution)/shard_map/ppermute | solution.py:34
  340.5 2.0 fusion.33
  342.5 2.3 reduce_sum.146
  344.8 3.6 %convolution_convert_fusion.7 = bf16[320,640]{1,0:T(8,128)(2,1)} fusion(bf16[1536,320]{1,0:T(8,128)(2,1)} %bitcast.6, bf16[1536,640]{1,0:T(8,128)(2,1)} %all-gather.10.cloned.1.call-done), kind=kOutput, calls=%fused_computation.36 | convolution fusion | flops 629350400 | bytes 3358720 | tf_op jit(solution)/shard_map/dot_general | solution.py:69
  351.1 2.3 slice_reduce_fusion
  (133 shorter events, 29.2 us)
Async XLA Ops:
  8.0 56.5 %copy-start = (bf16[1280,640]{1,0:T(8,128)(2,1)S(1)}, bf16[1280,640]{1,0:T(8,128)(2,1)}, u32[]{:S(2)}) copy-start(bf16[1280,640]{1,0:T(8,128)(2,1)} %param.27) | copy-start | bytes 4915204
  8.0 75.1 %reduce-scatter.2.cloned.1.call-start = ((), (), s32[]{:S(2)}) async-start(), calls=%async_computation.7 | async-start | bytes 11796480 | tf_op jit(solution)/shard_map/reduce_scatter | solution.py:142
  17.9 0.9 copy-start.20
  17.9 16.9 %copy-start.2 = (bf16[1,384,1280]{2,1,0:T(8,128)(2,1)S(1)}, bf16[1,384,1280]{2,1,0:T(8,128)(2,1)}, u32[]{:S(2)}) copy-start(bf16[1,384,1280]{2,1,0:T(8,128)(2,1)} %param.21) | copy-start | bytes 2949124
  17.9 150.0 %all-gather.6.cloned.1.call-start = ((), (), s32[]{:S(2)}) async-start(), calls=%async_computation.8 | async-start | bytes 11141120 | tf_op jit(solution)/shard_map/all_gather | solution.py:140
  34.8 3.2 copy-start.21
  37.0 1.1 copy-start.17
  42.2 34.4 %all-to-all-start = ((bf16[16,96,320]{2,1,0:T(8,128)(2,1)}), bf16[16,96,320]{2,1,0:T(8,128)(2,1)}, u32[]{:S(2)}, u32[]{:S(2)}) async-start(bf16[16,96,320]{2,1,0:T(8,128)(2,1)} %fusion.11), calls=%async_computation.1 | async-start | bytes 2359296 | tf_op jit(solution)/shard_map/all_to_all | solution.py:18
  54.7 3.7 %copy-start.23 = (s32[32]{0:T(128)S(1)}, s32[32]{0:T(128)}, u32[]{:S(2)}) copy-start(s32[32]{0:T(128)} %param.19) | copy-start | bytes 388
  54.7 4.0 %copy-start.14 = (bf16[1024,256]{1,0:T(8,128)(2,1)S(1)}, bf16[1024,256]{1,0:T(8,128)(2,1)}, u32[]{:S(2)}) copy-start(bf16[1024,256]{1,0:T(8,128)(2,1)} %hidden_ref.1) | copy-start | bytes 1572868
  56.5 3.2 copy-start.22
  58.7 8.1 %slice-start = ((s8[6553600]{0:T(1024)(128)(4,1)}), s8[4194304]{0:T(1024)(128)(4,1)S(1)}, s32[]{:S(2)}) async-start(s8[6553600]{0:T(1024)(128)(4,1)} %bitcast.89), calls=%async_computation.11 | async-start | bytes 8388608
  59.7 4.8 %copy-start.11 = (bf16[1,384,1280]{2,1,0:T(8,128)(2,1)S(1)}, bf16[1,384,1280]{2,1,0:T(8,128)(2,1)}, u32[]{:S(2)}) copy-start(bf16[1,384,1280]{2,1,0:T(8,128)(2,1)} %param.22) | copy-start | bytes 2949124
  59.7 4.8 %copy-start.25 = (f32[640]{0:T(1024)S(1)}, f32[640]{0:T(1024)}, u32[]{:S(2)}) copy-start(f32[640]{0:T(1024)} %param.28) | copy-start | bytes 7684
  62.9 3.9 %slice-start.1 = ((s8[6553600]{0:T(1024)(128)(4,1)}), s8[2359296]{0:T(1024)(128)(4,1)S(1)}, s32[]{:S(2)}) async-start(s8[6553600]{0:T(1024)(128)(4,1)} %bitcast.89), calls=%async_computation.12 | async-start | bytes 4718592
  64.5 2.3 copy-start.4
  64.5 2.7 copy-start.5
  64.5 3.6 copy-start.6
  89.6 49.5 %all-to-all-start.1 = ((bf16[16,96,640]{2,1,0:T(8,128)(2,1)}), bf16[16,96,640]{2,1,0:T(8,128)(2,1)}, u32[]{:S(2)}, u32[]{:S(2)}) async-start(bf16[16,96,640]{2,1,0:T(8,128)(2,1)} %bitcast.99), calls=%async_computation.2 | async-start | bytes 3932160 | tf_op jit(solution)/shard_map/all_to_all | solution.py:18
  96.7 161.2 %all-gather.8.cloned.1.call-start = ((), (), s32[]{:S(2)}) async-start(), calls=%async_computation.9 | async-start | bytes 2088960 | tf_op jit(solution)/shard_map/all_gather | solution.py:160
  162.0 6.0 %copy-start.10 = (bf16[96,640]{1,0:T(8,128)(2,1)}, bf16[96,640]{1,0:T(8,128)(2,1)S(1)}, u32[]{:S(2)}) copy-start(bf16[96,640]{1,0:T(8,128)(2,1)S(1)} %fusion.12) | copy-start | bytes 368644
  178.3 6.8 %copy-start.15 = (bf16[8,16,8,256]{3,2,0,1:T(8,128)(2,1)S(1)}, bf16[8,16,8,256]{3,2,0,1:T(8,128)(2,1)}, u32[]{:S(2)}) copy-start(bf16[8,16,8,256]{3,2,0,1:T(8,128)(2,1)} %copy.66) | copy-start | bytes 1572868
  180.8 17.9 %all-to-all-start.2 = ((bf16[8,48,1280]{2,1,0:T(8,128)(2,1)}), bf16[8,48,1280]{2,1,0:T(8,128)(2,1)S(1)}, u32[]{:S(2)}, u32[]{:S(2)}) async-start(bf16[8,48,1280]{2,1,0:T(8,128)(2,1)} %reshape.200), calls=%async_computation.3 | async-start | bytes 1966080 | tf_op jit(solution)/shard_map/all_to_all | solution.py:18
  184.4 160.4 %all-gather.10.cloned.1.call-start = ((), (), s32[]{:S(2)}) async-start(), calls=%async_computation.10 | async-start | bytes 2088960 | tf_op jit(solution)/shard_map/all_gather | solution.py:200
  216.0 30.7 %all-to-all-start.3 = ((bf16[16,96,320]{2,1,0:T(8,128)(2,1)}), bf16[16,96,320]{2,1,0:T(8,128)(2,1)}, u32[]{:S(2)}, u32[]{:S(2)}) async-start(bf16[16,96,320]{2,1,0:T(8,128)(2,1)} %copy.68), calls=%async_computation.4 | async-start | bytes 2359296 | tf_op jit(solution)/shard_map/all_to_all | solution.py:18
  225.5 2.1 copy-start.1
  227.7 1.5 copy-start.16
  228.2 1.0 copy-start.3
  246.6 32.6 %all-to-all-start.4 = ((bf16[16,40,1280]{2,1,0:T(8,128)(2,1)}), bf16[16,40,1280]{2,1,0:T(8,128)(2,1)}, u32[]{:S(2)}, u32[]{:S(2)}) async-start(bf16[16,40,1280]{2,1,0:T(8,128)(2,1)} %bitcast.96), calls=%async_computation.5 | async-start | bytes 3276800 | tf_op jit(solution)/shard_map/all_to_all | solution.py:18
  252.5 3.1 copy-start.12
  255.6 3.2 copy-start.7
  257.8 11.1 %copy-start.24 = (bf16[1536,640]{1,0:T(8,128)(2,1)S(1)}, bf16[1536,640]{1,0:T(8,128)(2,1)}, u32[]{:S(2)}) copy-start(bf16[1536,640]{1,0:T(8,128)(2,1)} %all-gather.8.cloned.1.call-done) | copy-start | bytes 5898244
  258.8 10.1 %copy-start.13 = (bf16[384,1280]{1,0:T(8,128)(2,1)}, bf16[384,1280]{1,0:T(8,128)(2,1)S(1)}, u32[]{:S(2)}) copy-start(bf16[384,1280]{1,0:T(8,128)(2,1)S(1)} %convolution_convert_fusion.5) | copy-start | bytes 2949124
  259.8 71.7 %collective-permute-start = (bf16[48,1280]{1,0:T(8,128)(2,1)}, bf16[48,1280]{1,0:T(8,128)(2,1)}, u32[]{:S(2)}, u32[]{:S(2)}) collective-permute-start(bf16[48,1280]{1,0:T(8,128)(2,1)} %get-tuple-element.78), channel_id=1, source_target_pairs={{0,16},{16,32},{32,48},{48,64},{64,80},{80,96},{96,112},{112,0},{1... | collective-permute-start | bytes 368648 | tf_op jit(solution)/shard_map/ppermute | solution.py:34
  261.6 70.1 %collective-permute-start.1 = (bf16[48,1280]{1,0:T(8,128)(2,1)}, bf16[48,1280]{1,0:T(8,128)(2,1)}, u32[]{:S(2)}, u32[]{:S(2)}) collective-permute-start(bf16[48,1280]{1,0:T(8,128)(2,1)} %get-tuple-element.84), channel_id=1, source_target_pairs={{0,32},{16,48},{32,64},{48,80},{64,96},{80,112},{96,0},{112,16},{1... | collective-permute-start | bytes 368648 | tf_op jit(solution)/shard_map/ppermute | solution.py:34
  263.0 72.7 %collective-permute-start.2 = (bf16[48,1280]{1,0:T(8,128)(2,1)}, bf16[48,1280]{1,0:T(8,128)(2,1)}, u32[]{:S(2)}, u32[]{:S(2)}) collective-permute-start(bf16[48,1280]{1,0:T(8,128)(2,1)} %get-tuple-element.83), channel_id=1, source_target_pairs={{0,48},{16,64},{32,80},{48,96},{64,112},{80,0},{96,16},{112,32},{1... | collective-permute-start | bytes 368648 | tf_op jit(solution)/shard_map/ppermute | solution.py:34
  264.3 71.3 %collective-permute-start.3 = (bf16[48,1280]{1,0:T(8,128)(2,1)}, bf16[48,1280]{1,0:T(8,128)(2,1)}, u32[]{:S(2)}, u32[]{:S(2)}) collective-permute-start(bf16[48,1280]{1,0:T(8,128)(2,1)} %get-tuple-element.82), channel_id=1, source_target_pairs={{0,64},{16,80},{32,96},{48,112},{64,0},{80,16},{96,32},{112,48},{1... | collective-permute-start | bytes 368648 | tf_op jit(solution)/shard_map/ppermute | solution.py:34
  266.3 69.4 %collective-permute-start.4 = (bf16[48,1280]{1,0:T(8,128)(2,1)}, bf16[48,1280]{1,0:T(8,128)(2,1)}, u32[]{:S(2)}, u32[]{:S(2)}) collective-permute-start(bf16[48,1280]{1,0:T(8,128)(2,1)} %get-tuple-element.81), channel_id=1, source_target_pairs={{0,80},{16,96},{32,112},{48,0},{64,16},{80,32},{96,48},{112,64},{1... | collective-permute-start | bytes 368648 | tf_op jit(solution)/shard_map/ppermute | solution.py:34
  272.7 3.6 copy-start.9
  279.3 7.1 %copy-start.8 = (bf16[384,640]{1,0:T(8,128)(2,1)S(1)}, bf16[384,640]{1,0:T(8,128)(2,1)}, u32[]{:S(2)}) copy-start(bf16[384,640]{1,0:T(8,128)(2,1)} %copy-done.7) | copy-start | bytes 1474564
  279.3 69.2 %all-to-all-start.5 = ((bf16[16,100,640]{2,1,0:T(8,128)(2,1)}), bf16[16,100,640]{2,1,0:T(8,128)(2,1)}, u32[]{:S(2)}, u32[]{:S(2)}) async-start(bf16[16,100,640]{2,1,0:T(8,128)(2,1)} %pad_maximum_fusion), calls=%async_computation.6 | async-start | bytes 4259840 | tf_op jit(solution)/shard_map/all_to_all | solution.py:18
  287.8 43.7 %copy-start.19 = (bf16[48,1280]{1,0:T(8,128)(2,1)S(1)}, bf16[48,1280]{1,0:T(8,128)(2,1)}, u32[]{:S(2)}) copy-start(bf16[48,1280]{1,0:T(8,128)(2,1)} %get-tuple-element.80) | copy-start | bytes 368644
  287.8 44.0 %copy-start.18 = (bf16[48,1280]{1,0:T(8,128)(2,1)S(1)}, bf16[48,1280]{1,0:T(8,128)(2,1)}, u32[]{:S(2)}) copy-start(bf16[48,1280]{1,0:T(8,128)(2,1)} %get-tuple-element.79) | copy-start | bytes 368644
  331.5 4.1 %collective-permute-start.5 = (bf16[48,1280]{1,0:T(8,128)(2,1)S(1)}, bf16[48,1280]{1,0:T(8,128)(2,1)S(1)}, u32[]{:S(2)}, u32[]{:S(2)}) collective-permute-start(bf16[48,1280]{1,0:T(8,128)(2,1)S(1)} %copy-done.19), channel_id=1, source_target_pairs={{0,96},{16,112},{32,0},{48,16},{64,32},{80,48},{96,64},{112,80},{1... | collective-permute-start | bytes 368648 | tf_op jit(solution)/shard_map/ppermute | solution.py:34
  331.8 8.7 %collective-permute-start.6 = (bf16[48,1280]{1,0:T(8,128)(2,1)S(1)}, bf16[48,1280]{1,0:T(8,128)(2,1)S(1)}, u32[]{:S(2)}, u32[]{:S(2)}) collective-permute-start(bf16[48,1280]{1,0:T(8,128)(2,1)S(1)} %copy-done.18), channel_id=1, source_target_pairs={{0,112},{16,0},{32,16},{48,32},{64,48},{80,64},{96,80},{112,96},{1... | collective-permute-start | bytes 368648 | tf_op jit(solution)/shard_map/ppermute | solution.py:34
Sparse Core Ops, SparseCore 0:
  18.0 65.0 reduce-scatter.1
Sparse Core Ops, SparseCore 1:
  34.9 114.2 all-gather.5
  151.8 43.1 all-gather.7
  197.6 53.6 all-gather.9
where the time goes:
time: 366 us; the launch traced here: 361 us
  blocking collectives  86 us (23%)
  waiting for transfers between devices  80.9 us (22%)
  starting transfers between devices  54.3 us (15%)
  matrix products  52.5 us (14%)
  local copies, waits for them, and re-layouts  33.8 us (9%)
  other arithmetic  27.4 us (7%)
  between operations  16.5 us (5%)
  Pallas kernels  9.83 us (3%)
    all_to_all x6, waiting for transfers between devices, exchanged(): return lax.all_to_all(pieces, axis, 0, 0, tiled=True)  68.4 us
    all_to_all x6, starting transfers between devices, exchanged(): return lax.all_to_all(pieces, axis, 0, 0, tiled=True)  41.6 us
    all_gather x1, blocking collectives, step(): sums = jnp.sum(lax.all_gather(sums, 'span', axis=0), axis=0)  39.4 us
    dot_general x5, matrix products, contract_first(): lax.dot_general(left, right, (((0,), (0,)), ((), ())), preferred_element_...  19.1 us
    all_gather x1, blocking collectives, step(): token_grad = lax.all_gather(token_block, 'seq', axis=1, tiled=True)  16 us
    all_gather x1, blocking collectives, step(): piece = lax.all_gather(llm_input, 'seq', axis=0, tiled=True)  16 us
    dot_general x4, matrix products, contract_last(): lax.dot_general(left, right, (((1,), (1,)), ((), ())), preferred_element_...  14.9 us
    all_gather x1, blocking collectives, step(): normed_grad = lax.all_gather(normed_mine, 'seq', axis=0, tiled=True)  14.5 us
  transfers between devices with their start and end apart: 17, of which 6 were waited for; matrix products, arithmetic and copies ran while one was open for 29% of the time, Pallas kernels for 0%

commit v1 on v0

--- a/solution.py
+++ b/solution.py
@@ -35,12 +35,7 @@
     total = mine.astype(jnp.float32)
     for piece in arrived:
         total = total + piece.astype(jnp.float32)
-    return total
-
-
-def blocks_swapped(array, outer, inner):
-    blocks = array.reshape(outer, inner, -1, array.shape[1])
-    return jnp.swapaxes(blocks, 0, 1).reshape(array.shape)
+    return total.astype(jnp.bfloat16)
 
 
 def gelu_value(values):
@@ -136,8 +131,7 @@
     total_slots = owner_count * slots_each
     mine_frames = frames_each // seq_size
 
-    piece = lax.all_gather(llm_input, "seq", axis=0, tiled=True)
-    piece = lax.all_gather(piece, "span", axis=0, tiled=True)
+    piece = lax.all_gather(llm_input, ("seq", "span"), axis=0, tiled=True)
     up_grad, blocks = column_blocks(hidden_grad, gate_act, up_weight, seq_size)
     partial_rows = lax.psum_scatter(
         blocks.reshape(seq_size * rows_all, blocks.shape[2]),
@@ -145,9 +139,6 @@
         scatter_dimension=0,
         tiled=True,
     )
-
-    hidden_rows = blocks_swapped(hidden_grad, seq_size, owner_count)
-    up_grad_rows = blocks_swapped(up_grad, seq_size, owner_count)
 
     slot_of = locate_rows(span_counts, row_ticks, capacity)
     matches = jnp.arange(total_slots, dtype=jnp.int32)[:, None] == slot_of[None, :]
@@ -174,8 +165,6 @@
         hidden_slope,
         nhat,
         rstd,
-        hidden_rows,
-        up_grad_rows,
     ) = lax.optimization_barrier(
         (
             partial_rows,
@@ -186,8 +175,6 @@
             hidden_slope,
             nhat,
             rstd,
-            hidden_rows,
-            up_grad_rows,
         )
     )
 
@@ -196,17 +183,16 @@
     token_grad = lax.all_gather(token_block, "seq", axis=1, tiled=True)
 
     pre_grad = (contract_last(token_grad, adapter_out) * act_slope).astype(jnp.bfloat16)
+    pre_grad_all = lax.all_gather(pre_grad, "span", axis=0, tiled=True)
     normed_part = contract_last(pre_grad, adapter_in).astype(jnp.bfloat16)
-    pre_grad_all = lax.all_gather(pre_grad, "span", axis=0, tiled=True)
     normed_part, token_grad, piece = lax.optimization_barrier((normed_part, token_grad, piece))
     normed_pieces = exchanged(normed_part.reshape(seq_size, mine_frames, width), "seq")
 
     token_cols = jnp.moveaxis(token_grad.reshape(slots_each, owner_count, -1), 1, 0)
 
     up_rows = jnp.dot(piece, up_weight, preferred_element_type=jnp.float32)
-    gate_rows = (hidden_rows.astype(jnp.float32) * up_rows).astype(jnp.bfloat16)
-    gate_act_grad = blocks_swapped(gate_rows, owner_count, seq_size)
-    up_weight_grad = contract_first(piece, up_grad_rows).astype(jnp.bfloat16)
+    gate_act_grad = (hidden_grad.astype(jnp.float32) * up_rows).astype(jnp.bfloat16)
+    up_weight_grad = contract_first(piece, up_grad).astype(jnp.bfloat16)
     normed_pieces, gate_act_grad, up_weight_grad, token_cols = lax.optimization_barrier(
         (normed_pieces, gate_act_grad, up_weight_grad, token_cols)
     )
@@ -235,42 +221,47 @@
     mlp_part, hidden_pre_grad, columns, normed_grad = lax.optimization_barrier(
         (mlp_part, hidden_pre_grad, columns, normed_grad)
     )
+
+    frame_grad = normed_grad.astype(jnp.float32)
+    sums = jnp.concatenate(
+        [
+            jnp.sum(frame_grad * nhat, axis=0),
+            jnp.sum(frame_grad, axis=0),
+            jnp.sum(resid.astype(jnp.float32), axis=0),
+            jnp.sum(hidden_pre_grad.astype(jnp.float32), axis=0),
+        ]
+    ).reshape(-1, expand_part.shape[1])
+    high = lax.reduce_precision(sums, exponent_bits=8, mantissa_bits=7)
+    halves = jnp.concatenate([high, sums - high]).astype(jnp.bfloat16)
     rows = expand_part.shape[0] // owner_count
+    out_pieces = out_part.reshape(owner_count, -1, expand_part.shape[1])
     packed = jnp.concatenate(
         [
             expand_part.reshape(owner_count, rows, -1),
-            out_part.reshape(owner_count, -1, expand_part.shape[1]),
+            out_pieces,
+            jnp.broadcast_to(halves, (owner_count, *halves.shape)),
         ],
         axis=1,
     )
     packed, contract_pieces = lax.optimization_barrier((packed, contract_pieces))
     packed = exchanged(packed, "span")
     contract_weight_grad = jnp.sum(contract_pieces.astype(jnp.float32), axis=0).astype(jnp.bfloat16)
-    mlp_input_grad = permuted_sum(
-        mlp_part.reshape(seq_size, mine_frames, width), "seq"
-    ).astype(jnp.bfloat16)
+    mlp_input_grad = permuted_sum(mlp_part.reshape(seq_size, mine_frames, width), "seq")
 
     adapter_in_grad = contract_first(columns, pre_grad_all).astype(jnp.bfloat16)
 
-    normed_grad = normed_grad.astype(jnp.float32)
-    sums = jnp.concatenate(
-        [
-            jnp.sum(normed_grad * nhat, axis=0),
-            jnp.sum(normed_grad, axis=0),
-            jnp.sum(resid.astype(jnp.float32), axis=0),
-            jnp.sum(hidden_pre_grad.astype(jnp.float32), axis=0),
-        ]
-    )
-    sums = jnp.sum(lax.all_gather(sums, "span", axis=0), axis=0)
+    expand_weight_grad = jnp.sum(packed[:, :rows].astype(jnp.float32), axis=0).astype(jnp.bfloat16)
+    out_end = rows + out_pieces.shape[1]
+    out_rows = packed[:, rows:out_end].reshape(owner_count, -1, out_part.shape[1])
+    adapter_out_grad = jnp.moveaxis(out_rows, 0, 1).reshape(out_rows.shape[1], -1)
+    sums = jnp.sum(packed[:, out_end:].astype(jnp.float32), axis=0)
+    sums = (sums[: high.shape[0]] + sums[high.shape[0] :]).reshape(-1)
     post_gain_grad, post_bias_grad, contract_bias_grad, expand_bias_grad = (
         sums[:width],
         sums[width : 2 * width],
         sums[2 * width : 3 * width],
         sums[3 * width :],
     )
-    expand_weight_grad = jnp.sum(packed[:, :rows].astype(jnp.float32), axis=0).astype(jnp.bfloat16)
-    out_rows = packed[:, rows:].reshape(owner_count, -1, out_part.shape[1])
-    adapter_out_grad = jnp.moveaxis(out_rows, 0, 1).reshape(out_rows.shape[1], -1)
     resid_mine = lax.dynamic_slice_in_dim(resid, seq_index * mine_frames, mine_frames, 0)
     return (
         gate_act_grad,

time: 366 us -> 322 us (0.88)
  the two profiles are of different devices: /device:TPU:1 before, /device:TPU:0 now
where the time goes in v1:
time: 322 us; the launch traced here: 320 us
  waiting for transfers between devices  107 us (33%)
  matrix products  58.1 us (18%)
  starting transfers between devices  44.7 us (14%)
  local copies, waits for them, and re-layouts  28.7 us (9%)
  blocking collectives  28.3 us (9%)
  other arithmetic  27.7 us (9%)
  between operations  16.2 us (5%)
  Pallas kernels  9.83 us (3%)
    all_to_all x6, waiting for transfers between devices, exchanged(): return lax.all_to_all(pieces, axis, 0, 0, tiled=True)  71.1 us
    all_to_all x6, starting transfers between devices, exchanged(): return lax.all_to_all(pieces, axis, 0, 0, tiled=True)  34.4 us
    reduce_scatter x1, waiting for transfers between devices, step(): lax.psum_scatter(blocks.reshape(seq_size * rows_all, blocks.shape[2]), 's...  31.6 us
    dot_general x5, matrix products, contract_first(): lax.dot_general(left, right, (((0,), (0,)), ((), ())), preferred_element_...  19.2 us
    dot_general x4, matrix products, contract_last(): lax.dot_general(left, right, (((1,), (1,)), ((), ())), preferred_element_...  15.9 us
    all_gather x1, blocking collectives, step(): normed_grad = lax.all_gather(normed_mine, 'seq', axis=0, tiled=True)  14.3 us
    all_gather x1, blocking collectives, step(): token_grad = lax.all_gather(token_block, 'seq', axis=1, tiled=True)  14 us
    ppermute x7, starting transfers between devices, permuted_sum(): lax.ppermute(piece, axis, [(i, (i + step) % size) for i in range(size)])  10.1 us
  transfers between devices with their start and end apart: 17, of which 9 were waited for; matrix products, arithmetic and copies ran while one was open for 33% of the time, Pallas kernels for 0%

profile of v1, /device:TPU:0, one launch (start us, length us, event | category | flops | bytes accessed | tf_op | source)
XLA Modules:
  0.0 320.3 jit_solution(10880245495421503231)
XLA Ops:
  8.1 9.8 %column_blocks.1 = (bf16[1024,256]{1,0:T(8,128)(2,1)}, bf16[8,1024,640]{2,1,0:T(8,128)(2,1)}) custom-call(bf16[1024,256]{1,0:T(8,128)(2,1)} %hidden_ref.1, bf16[1024,256]{1,0:T(8,128)(2,1)} %gate_ref.1, bf16[5120,256]{1,0:T(8,128)(2,1)} %weight_ref.1), custom_call_target="tpu_custom_call" | custom-call | flops 2684354560 | bytes 14680064 | tf_op jit(solution)/shard_map/column_blocks/pallas_call | solution.py:82
  19.1 2.2 reshape.199
  22.5 3.8 %fusion.11 = bf16[16,96,320]{2,1,0:T(8,128)(2,1)} fusion(f32[96,16,320]{2,1,0:T(8,128)} %reshape.199, f32[16,320]{1,0:T(8,128)S(1)} %add.175, f32[16,320]{1,0:T(8,128)S(1)} %mul.187, f32[96,16]{0,1:T(8,128)S(1)} %bitcast.89, f32[96,16]{0,1:T(8,128)S(1)} %bitcast.90), kind=kLoop, calls=%fused_computation.37 | loop fusion | flops 2457600 | bytes 3002368 | tf_op jit(solution)/shard_map/transpose | solution.py:153
  26.3 8.2 %all-to-all-start = ((bf16[16,96,320]{2,1,0:T(8,128)(2,1)}), bf16[16,96,320]{2,1,0:T(8,128)(2,1)}, u32[]{:S(2)}, u32[]{:S(2)}) async-start(bf16[16,96,320]{2,1,0:T(8,128)(2,1)} %fusion.11), calls=%async_computation.1 | async-start | bytes 2359296 | tf_op jit(solution)/shard_map/all_to_all | solution.py:18
  34.6 1.8 reshape.198
  36.7 1.6 copy.59
  38.7 1.6 copy.58
  40.4 6.9 %multiply_convert_fusion.2 = (bf16[96,640]{1,0:T(8,128)(2,1)}, f32[96,640]{1,0:T(8,128)S(1)}) fusion(bf16[5120,640]{1,0:T(8,128)(2,1)} %param.25, f32[96,5120]{1,0:T(8,128)} %bitcast.78, f32[96,5120]{1,0:T(8,128)} %reshape.198, f32[96,5120]{1,0:T(8,128)} %bitcast.79, f32[5120]{0:T(1024)S(1)} %add.168, f32[5120]{0:T(1024)S(1)} %mul.170), kind=kOutput, calls=%fused_computation.66 | convolution fusion | flops 632279040 | bytes 12861440 | tf_op jit(solution)/shard_map/dot_general | solution.py:148
  47.7 3.2 fusion
  50.9 2.3 fusion.16
  53.2 1.6 fusion.8
  54.7 31.6 %reduce-scatter.2.cloned.1.call-done = bf16[1024,640]{1,0:T(8,128)(2,1)} async-done(((bf16[8192,640]{1,0:T(8,128)(2,1)}), bf16[1024,640]{1,0:T(8,128)(2,1)}) %reduce-scatter.2.cloned.1.call-update) | async-done | bytes 1310736 | tf_op jit(solution)/shard_map/reduce_scatter | solution.py:136
  86.3 6.2 %convolution_convert_fusion.2 = bf16[1536,640]{1,0:T(8,128)(2,1)} fusion(bf16[1536,1024]{1,0:T(8,128)(2,1)} %fusion, bf16[1024,640]{1,0:T(8,128)(2,1)} %reduce-scatter.2.cloned.1.call-done), kind=kOutput, calls=%fused_computation.4 | convolution fusion | flops 2014248960 | bytes 6422528 | tf_op jit(solution)/shard_map/dot_general | solution.py:181
  92.5 7.6 %all-to-all-start.1 = ((bf16[16,96,640]{2,1,0:T(8,128)(2,1)}), bf16[16,96,640]{2,1,0:T(8,128)(2,1)}, u32[]{:S(2)}, u32[]{:S(2)}) async-start(bf16[16,96,640]{2,1,0:T(8,128)(2,1)} %bitcast.85), calls=%async_computation.2 | async-start | bytes 3932160 | tf_op jit(solution)/shard_map/all_to_all | solution.py:18
  100.1 37.5 %all-to-all-done.1 = bf16[16,96,640]{2,1,0:T(8,128)(2,1)} async-done(((bf16[16,96,640]{2,1,0:T(8,128)(2,1)}), bf16[16,96,640]{2,1,0:T(8,128)(2,1)}, u32[]{:S(2)}, u32[]{:S(2)}) %all-to-all-start.1) | async-done | bytes 1966112 | tf_op jit(solution)/shard_map/all_to_all | solution.py:18
  137.5 1.8 reduce_sum.141
  139.4 14.0 %all_gather.15 = bf16[96,5120]{1,0:T(8,128)(2,1)S(1)} all-gather(bf16[96,640]{1,0:T(8,128)(2,1)S(1)} %reduce_sum.141), channel_id=1, replica_groups=mesh['seq'=8,'span'=16] {'seq'}, dimensions={1}, use_global_device_ids=true | all-gather | bytes 1105920 | tf_op jit(solution)/shard_map/all_gather | solution.py:183
  153.4 4.9 %fusion.12 = bf16[96,640]{1,0:T(8,128)(2,1)S(1)} fusion(f32[96,640]{1,0:T(8,128)S(1)} %get-tuple-element.44, bf16[96,5120]{1,0:T(8,128)(2,1)S(1)} %all_gather.15, bf16[640,5120]{1,0:T(8,128)(2,1)} %param.26), kind=kOutput, calls=%fused_computation.39 | convolution fusion | flops 629268480 | bytes 7905280 | tf_op jit(solution)/shard_map/dot_general | solution.py:58
  158.4 6.0 %convolution_convert_fusion.1 = bf16[96,5120]{1,0:T(8,128)(2,1)} fusion(bf16[96,640]{1,0:T(8,128)(2,1)S(1)} %fusion.12, bf16[5120,640]{1,0:T(8,128)(2,1)} %param.25), kind=kOutput, calls=%fused_computation.3 | convolution fusion | flops 629637120 | bytes 7659520 | tf_op jit(solution)/shard_map/dot_general | solution.py:58
  164.3 1.8 reshape.187
  166.1 2.5 reshape.186
  168.6 3.6 %all-to-all-start.2 = ((bf16[8,48,1280]{2,1,0:T(8,128)(2,1)}), bf16[8,48,1280]{2,1,0:T(8,128)(2,1)S(1)}, u32[]{:S(2)}, u32[]{:S(2)}) async-start(bf16[8,48,1280]{2,1,0:T(8,128)(2,1)} %reshape.186), calls=%async_computation.3 | async-start | bytes 1966080 | tf_op jit(solution)/shard_map/all_to_all | solution.py:18
  172.8 8.8 %convolution_convert_fusion = bf16[5120,256]{1,0:T(8,128)(2,1)} fusion(bf16[1024,5120]{1,0:T(8,128)(2,1)} %all-gather.4.cloned.1.call-done, bf16[1024,256]{1,0:T(8,128)(2,1)S(1)} %copy-done.18), kind=kOutput, calls=%fused_computation | convolution fusion | flops 2685665280 | bytes 13631488 | tf_op jit(solution)/shard_map/dot_general | solution.py:64
  181.6 7.7 %fusion.9 = bf16[1024,256]{1,0:T(8,128)(2,1)} fusion(bf16[1024,5120]{1,0:T(8,128)(2,1)} %all-gather.4.cloned.1.call-done, bf16[5120,256]{1,0:T(8,128)(2,1)S(1)} %copy-done.14, bf16[1024,256]{1,0:T(8,128)(2,1)S(1)} %copy-done.16), kind=kOutput, calls=%fused_computation.33 | convolution fusion | flops 2685140992 | bytes 14155776 | tf_op jit(solution)/shard_map/dot_general | solution.py:193
  189.4 14.3 %all_gather.17 = bf16[384,1280]{1,0:T(8,128)(2,1)S(1)} all-gather(bf16[48,1280]{1,0:T(8,128)(2,1)S(1)} %reduce_sum.142), channel_id=1, replica_groups=mesh['seq'=8,'span'=16] {'seq'}, dimensions={0}, use_global_device_ids=true | all-gather | bytes 1105920 | tf_op jit(solution)/shard_map/all_gather | solution.py:202
  203.7 2.5 copy.54
  206.3 5.3 %all-to-all-start.3 = ((bf16[16,96,320]{2,1,0:T(8,128)(2,1)}), bf16[16,96,320]{2,1,0:T(8,128)(2,1)}, u32[]{:S(2)}, u32[]{:S(2)}) async-start(bf16[16,96,320]{2,1,0:T(8,128)(2,1)} %copy.54), calls=%async_computation.4 | async-start | bytes 2359296 | tf_op jit(solution)/shard_map/all_to_all | solution.py:18
  211.6 2.1 fusion.7
  215.2 2.2 convolution_convert_fusion.4
  217.4 18.1 %all-to-all-done.3 = bf16[16,96,320]{2,1,0:T(8,128)(2,1)} async-done(((bf16[16,96,320]{2,1,0:T(8,128)(2,1)}), bf16[16,96,320]{2,1,0:T(8,128)(2,1)}, u32[]{:S(2)}, u32[]{:S(2)}) %all-to-all-start.3) | async-done | bytes 983072 | tf_op jit(solution)/shard_map/all_to_all | solution.py:18
  235.5 3.0 fusion.10
  238.5 2.2 fusion.1
  240.7 5.4 %all-to-all-start.4 = ((bf16[16,40,1280]{2,1,0:T(8,128)(2,1)}), bf16[16,40,1280]{2,1,0:T(8,128)(2,1)}, u32[]{:S(2)}, u32[]{:S(2)}) async-start(bf16[16,40,1280]{2,1,0:T(8,128)(2,1)} %bitcast.82), calls=%async_computation.5 | async-start | bytes 3276800 | tf_op jit(solution)/shard_map/all_to_all | solution.py:18
  246.1 2.0 convolution_convert_fusion.5
  248.1 2.3 convolution_convert_fusion.6
  254.4 1.9 fusion.6
  256.2 2.9 copy.55
  259.2 2.8 pad_maximum_fusion
  261.9 6.6 %all-to-all-done.4 = bf16[16,40,1280]{2,1,0:T(8,128)(2,1)} async-done(((bf16[16,40,1280]{2,1,0:T(8,128)(2,1)}), bf16[16,40,1280]{2,1,0:T(8,128)(2,1)}, u32[]{:S(2)}, u32[]{:S(2)}) %all-to-all-start.4) | async-done | bytes 1638432 | tf_op jit(solution)/shard_map/all_to_all | solution.py:18
  268.5 4.5 %all-to-all-start.5 = ((bf16[16,114,640]{2,1,0:T(8,128)(2,1)}), bf16[16,114,640]{2,1,0:T(8,128)(2,1)}, u32[]{:S(2)}, u32[]{:S(2)}) async-start(bf16[16,114,640]{2,1,0:T(8,128)(2,1)} %pad_maximum_fusion), calls=%async_computation.6 | async-start | bytes 4915200 | tf_op jit(solution)/shard_map/all_to_all | solution.py:18
  275.0 2.1 collective-permute-start.2
  277.1 2.1 collective-permute-start.3
  281.5 2.5 collective-permute-start.6
  283.9 1.6 dynamic-slice_bitcast_fusion.7
  289.2 2.3 reduce_sum.150
  291.5 3.6 %convolution_convert_fusion.7 = bf16[320,640]{1,0:T(8,128)(2,1)} fusion(bf16[1536,320]{1,0:T(8,128)(2,1)} %bitcast.6, bf16[1536,640]{1,0:T(8,128)(2,1)} %all-gather.8.cloned.1.call-done), kind=kOutput, calls=%fused_computation.36 | convolution fusion | flops 629350400 | bytes 3358720 | tf_op jit(solution)/shard_map/dot_general | solution.py:64
  295.2 9.0 %all-to-all-done.5 = bf16[16,114,640]{2,1,0:T(8,128)(2,1)} async-done(((bf16[16,114,640]{2,1,0:T(8,128)(2,1)}), bf16[16,114,640]{2,1,0:T(8,128)(2,1)}, u32[]{:S(2)}, u32[]{:S(2)}) %all-to-all-start.5) | async-done | bytes 2334752 | tf_op jit(solution)/shard_map/all_to_all | solution.py:18
  310.4 2.3 slice_reduce_fusion
  (116 shorter events, 23.9 us)
Async XLA Ops:
  8.0 42.9 %copy-start = (bf16[1280,640]{1,0:T(8,128)(2,1)S(1)}, bf16[1280,640]{1,0:T(8,128)(2,1)}, u32[]{:S(2)}) copy-start(bf16[1280,640]{1,0:T(8,128)(2,1)} %param.27) | copy-start | bytes 4915204
  8.0 78.3 %reduce-scatter.2.cloned.1.call-start = ((), (), s32[]{:S(2)}) async-start(), calls=%async_computation.7 | async-start | bytes 11796480 | tf_op jit(solution)/shard_map/reduce_scatter | solution.py:136
  17.9 1.2 copy-start.2
  17.9 146.4 %all-gather.4.cloned.1.call-start = ((), (), s32[]{:S(2)}) async-start(), calls=%async_computation.8 | async-start | bytes 10567680 | tf_op jit(solution)/shard_map/all_gather | solution.py:134
  19.1 3.2 copy-start.11
  21.3 1.1 copy-start.10
  26.3 28.4 %all-to-all-start = ((bf16[16,96,320]{2,1,0:T(8,128)(2,1)}), bf16[16,96,320]{2,1,0:T(8,128)(2,1)}, u32[]{:S(2)}, u32[]{:S(2)}) async-start(bf16[16,96,320]{2,1,0:T(8,128)(2,1)} %fusion.11), calls=%async_computation.1 | async-start | bytes 2359296 | tf_op jit(solution)/shard_map/all_to_all | solution.py:18
  34.5 206.2 %all-gather.6.cloned.1.call-start = ((), (), s32[]{:S(2)}) async-start(), calls=%async_computation.9 | async-start | bytes 2088960 | tf_op jit(solution)/shard_map/all_gather | solution.py:151
  40.3 7.0 %copy-start.13 = (s32[32]{0:T(128)S(1)}, s32[32]{0:T(128)}, u32[]{:S(2)}) copy-start(s32[32]{0:T(128)} %param.19) | copy-start | bytes 388
  40.4 7.3 %copy-start.12 = (s32[1024]{0:T(1024)S(1)}, s32[1024]{0:T(1024)}, u32[]{:S(2)}) copy-start(s32[1024]{0:T(1024)} %param.20) | copy-start | bytes 12292
  47.3 3.6 %copy-start.17 = (f32[640]{0:T(1024)S(1)}, f32[640]{0:T(1024)}, u32[]{:S(2)}) copy-start(f32[640]{0:T(1024)} %param.28) | copy-start | bytes 7684
  47.6 3.3 %copy-start.6 = (bf16[1,384,1280]{2,1,0:T(8,128)(2,1)S(1)}, bf16[1,384,1280]{2,1,0:T(8,128)(2,1)}, u32[]{:S(2)}) copy-start(bf16[1,384,1280]{2,1,0:T(8,128)(2,1)} %param.22) | copy-start | bytes 2949124
  92.5 45.1 %all-to-all-start.1 = ((bf16[16,96,640]{2,1,0:T(8,128)(2,1)}), bf16[16,96,640]{2,1,0:T(8,128)(2,1)}, u32[]{:S(2)}, u32[]{:S(2)}) async-start(bf16[16,96,640]{2,1,0:T(8,128)(2,1)} %bitcast.85), calls=%async_computation.2 | async-start | bytes 3932160 | tf_op jit(solution)/shard_map/all_to_all | solution.py:18
  158.3 6.0 %copy-start.5 = (bf16[96,640]{1,0:T(8,128)(2,1)}, bf16[96,640]{1,0:T(8,128)(2,1)S(1)}, u32[]{:S(2)}) copy-start(bf16[96,640]{1,0:T(8,128)(2,1)S(1)} %fusion.12) | copy-start | bytes 368644
  166.1 6.7 %copy-start.18 = (bf16[1024,256]{1,0:T(8,128)(2,1)S(1)}, bf16[1024,256]{1,0:T(8,128)(2,1)}, u32[]{:S(2)}) copy-start(bf16[1024,256]{1,0:T(8,128)(2,1)} %get-tuple-element.47) | copy-start | bytes 1572868
  168.6 20.7 %all-to-all-start.2 = ((bf16[8,48,1280]{2,1,0:T(8,128)(2,1)}), bf16[8,48,1280]{2,1,0:T(8,128)(2,1)S(1)}, u32[]{:S(2)}, u32[]{:S(2)}) async-start(bf16[8,48,1280]{2,1,0:T(8,128)(2,1)} %reshape.186), calls=%async_computation.3 | async-start | bytes 1966080 | tf_op jit(solution)/shard_map/all_to_all | solution.py:18
  172.1 119.4 %all-gather.8.cloned.1.call-start = ((), (), s32[]{:S(2)}) async-start(), calls=%async_computation.10 | async-start | bytes 2088960 | tf_op jit(solution)/shard_map/all_gather | solution.py:186
  172.7 8.9 %copy-start.14 = (bf16[5120,256]{1,0:T(8,128)(2,1)S(1)}, bf16[5120,256]{1,0:T(8,128)(2,1)}, u32[]{:S(2)}) copy-start(bf16[5120,256]{1,0:T(8,128)(2,1)} %weight_ref.1) | copy-start | bytes 7864324
  172.7 8.9 %copy-start.16 = (bf16[1024,256]{1,0:T(8,128)(2,1)S(1)}, bf16[1024,256]{1,0:T(8,128)(2,1)}, u32[]{:S(2)}) copy-start(bf16[1024,256]{1,0:T(8,128)(2,1)} %hidden_ref.1) | copy-start | bytes 1572868
  206.3 29.2 %all-to-all-start.3 = ((bf16[16,96,320]{2,1,0:T(8,128)(2,1)}), bf16[16,96,320]{2,1,0:T(8,128)(2,1)}, u32[]{:S(2)}, u32[]{:S(2)}) async-start(bf16[16,96,320]{2,1,0:T(8,128)(2,1)} %copy.54), calls=%async_computation.4 | async-start | bytes 2359296 | tf_op jit(solution)/shard_map/all_to_all | solution.py:18
  211.5 2.1 copy-start.1
  213.7 1.5 copy-start.9
  214.2 1.0 copy-start.3
  235.5 3.0 copy-start.7
  238.5 7.6 %copy-start.4 = (bf16[384,640]{1,0:T(8,128)(2,1)}, bf16[384,640]{1,0:T(8,128)(2,1)S(1)}, u32[]{:S(2)}) copy-start(bf16[384,640]{1,0:T(8,128)(2,1)S(1)} %fusion.10) | copy-start | bytes 1474564
  240.7 27.7 %all-to-all-start.4 = ((bf16[16,40,1280]{2,1,0:T(8,128)(2,1)}), bf16[16,40,1280]{2,1,0:T(8,128)(2,1)}, u32[]{:S(2)}, u32[]{:S(2)}) async-start(bf16[16,40,1280]{2,1,0:T(8,128)(2,1)} %bitcast.82), calls=%async_computation.5 | async-start | bytes 3276800 | tf_op jit(solution)/shard_map/all_to_all | solution.py:18
  246.1 2.0 copy-start.15
  261.9 11.1 %copy-start.8 = (bf16[384,1280]{1,0:T(8,128)(2,1)S(1)}, bf16[384,1280]{1,0:T(8,128)(2,1)}, u32[]{:S(2)}) copy-start(bf16[384,1280]{1,0:T(8,128)(2,1)} %convolution_convert_fusion.5) | copy-start | bytes 2949124
  268.5 35.7 %all-to-all-start.5 = ((bf16[16,114,640]{2,1,0:T(8,128)(2,1)}), bf16[16,114,640]{2,1,0:T(8,128)(2,1)}, u32[]{:S(2)}, u32[]{:S(2)}) async-start(bf16[16,114,640]{2,1,0:T(8,128)(2,1)} %pad_maximum_fusion), calls=%async_computation.6 | async-start | bytes 4915200 | tf_op jit(solution)/shard_map/all_to_all | solution.py:18
  273.8 6.8 %collective-permute-start = (bf16[48,1280]{1,0:T(8,128)(2,1)}, bf16[48,1280]{1,0:T(8,128)(2,1)S(1)}, u32[]{:S(2)}, u32[]{:S(2)}) collective-permute-start(bf16[48,1280]{1,0:T(8,128)(2,1)} %get-tuple-element.74), channel_id=1, source_target_pairs={{0,16},{16,32},{32,48},{48,64},{64,80},{80,96},{96,112},{112,0},{1... | collective-permute-start | bytes 368648 | tf_op jit(solution)/shard_map/ppermute | solution.py:34
  273.8 7.6 %collective-permute-start.1 = (bf16[48,1280]{1,0:T(8,128)(2,1)}, bf16[48,1280]{1,0:T(8,128)(2,1)S(1)}, u32[]{:S(2)}, u32[]{:S(2)}) collective-permute-start(bf16[48,1280]{1,0:T(8,128)(2,1)} %get-tuple-element.80), channel_id=1, source_target_pairs={{0,32},{16,48},{32,64},{48,80},{64,96},{80,112},{96,0},{112,16},{1... | collective-permute-start | bytes 368648 | tf_op jit(solution)/shard_map/ppermute | solution.py:34
  275.0 11.2 %collective-permute-start.2 = (bf16[48,1280]{1,0:T(8,128)(2,1)S(1)}, bf16[48,1280]{1,0:T(8,128)(2,1)S(1)}, u32[]{:S(2)}, u32[]{:S(2)}) collective-permute-start(bf16[48,1280]{1,0:T(8,128)(2,1)S(1)} %get-tuple-element.79), channel_id=1, source_target_pairs={{0,48},{16,64},{32,80},{48,96},{64,112},{80,0},{96,16},{112,32},{1... | collective-permute-start | bytes 368648 | tf_op jit(solution)/shard_map/ppermute | solution.py:34
  277.1 10.2 %collective-permute-start.3 = (bf16[48,1280]{1,0:T(8,128)(2,1)S(1)}, bf16[48,1280]{1,0:T(8,128)(2,1)S(1)}, u32[]{:S(2)}, u32[]{:S(2)}) collective-permute-start(bf16[48,1280]{1,0:T(8,128)(2,1)S(1)} %get-tuple-element.78), channel_id=1, source_target_pairs={{0,64},{16,80},{32,96},{48,112},{64,0},{80,16},{96,32},{112,48},{1... | collective-permute-start | bytes 368648 | tf_op jit(solution)/shard_map/ppermute | solution.py:34
  279.1 8.2 %collective-permute-start.4 = (bf16[48,1280]{1,0:T(8,128)(2,1)S(1)}, bf16[48,1280]{1,0:T(8,128)(2,1)S(1)}, u32[]{:S(2)}, u32[]{:S(2)}) collective-permute-start(bf16[48,1280]{1,0:T(8,128)(2,1)S(1)} %get-tuple-element.77), channel_id=1, source_target_pairs={{0,80},{16,96},{32,112},{48,0},{64,16},{80,32},{96,48},{112,64},{1... | collective-permute-start | bytes 368648 | tf_op jit(solution)/shard_map/ppermute | solution.py:34
  280.7 7.4 %collective-permute-start.5 = (bf16[48,1280]{1,0:T(8,128)(2,1)S(1)}, bf16[48,1280]{1,0:T(8,128)(2,1)S(1)}, u32[]{:S(2)}, u32[]{:S(2)}) collective-permute-start(bf16[48,1280]{1,0:T(8,128)(2,1)S(1)} %get-tuple-element.76), channel_id=1, source_target_pairs={{0,96},{16,112},{32,0},{48,16},{64,32},{80,48},{96,64},{112,80},{1... | collective-permute-start | bytes 368648 | tf_op jit(solution)/shard_map/ppermute | solution.py:34
  281.5 6.9 %collective-permute-start.6 = (bf16[48,1280]{1,0:T(8,128)(2,1)S(1)}, bf16[48,1280]{1,0:T(8,128)(2,1)S(1)}, u32[]{:S(2)}, u32[]{:S(2)}) collective-permute-start(bf16[48,1280]{1,0:T(8,128)(2,1)S(1)} %get-tuple-element.75), channel_id=1, source_target_pairs={{0,112},{16,0},{32,16},{48,32},{64,48},{80,64},{96,80},{112,96},{1... | collective-permute-start | bytes 368648 | tf_op jit(solution)/shard_map/ppermute | solution.py:34
Sparse Core Ops, SparseCore 0:
  18.1 68.2 reduce-scatter.1
Sparse Core Ops, SparseCore 1:
  21.4 114.2 all-gather.3
  138.3 44.8 all-gather.5
  185.7 52.1 all-gather.7

commit v2 on v1

--- a/solution.py
+++ b/solution.py
@@ -131,7 +131,6 @@
     total_slots = owner_count * slots_each
     mine_frames = frames_each // seq_size
 
-    piece = lax.all_gather(llm_input, ("seq", "span"), axis=0, tiled=True)
     up_grad, blocks = column_blocks(hidden_grad, gate_act, up_weight, seq_size)
     partial_rows = lax.psum_scatter(
         blocks.reshape(seq_size * rows_all, blocks.shape[2]),
@@ -180,12 +179,14 @@
 
     partial_slots = jnp.dot(placing, partial_rows, preferred_element_type=jnp.float32)
     token_block = sent_and_summed(partial_slots.astype(jnp.bfloat16), "span").astype(jnp.bfloat16)
+    token_block, llm_input = lax.optimization_barrier((token_block, llm_input))
+    piece = lax.all_gather(llm_input, ("seq", "span"), axis=0, tiled=True)
     token_grad = lax.all_gather(token_block, "seq", axis=1, tiled=True)
 
     pre_grad = (contract_last(token_grad, adapter_out) * act_slope).astype(jnp.bfloat16)
     pre_grad_all = lax.all_gather(pre_grad, "span", axis=0, tiled=True)
     normed_part = contract_last(pre_grad, adapter_in).astype(jnp.bfloat16)
-    normed_part, token_grad, piece = lax.optimization_barrier((normed_part, token_grad, piece))
+    normed_part, token_grad = lax.optimization_barrier((normed_part, token_grad))
     normed_pieces = exchanged(normed_part.reshape(seq_size, mine_frames, width), "seq")
 
     token_cols = jnp.moveaxis(token_grad.reshape(slots_each, owner_count, -1), 1, 0)
@@ -193,9 +194,7 @@
     up_rows = jnp.dot(piece, up_weight, preferred_element_type=jnp.float32)
     gate_act_grad = (hidden_grad.astype(jnp.float32) * up_rows).astype(jnp.bfloat16)
     up_weight_grad = contract_first(piece, up_grad).astype(jnp.bfloat16)
-    normed_pieces, gate_act_grad, up_weight_grad, token_cols = lax.optimization_barrier(
-        (normed_pieces, gate_act_grad, up_weight_grad, token_cols)
-    )
+    normed_pieces, token_cols = lax.optimization_barrier((normed_pieces, token_cols))
     token_cols = exchanged(token_cols, "span").reshape(total_slots, -1)
 
     normed_mine = jnp.sum(normed_pieces.astype(jnp.float32), axis=0).astype(jnp.bfloat16)

time: 322 us -> 316 us (0.981)
  the two profiles are of different devices: /device:TPU:0 before, /device:TPU:1 now
where the time goes in v2:
time: 316 us; the launch traced here: 314 us
  waiting for transfers between devices  76.8 us (24%)
  blocking collectives  62.5 us (20%)
  matrix products  53.9 us (17%)
  starting transfers between devices  37.1 us (12%)
  local copies, waits for them, and re-layouts  29.2 us (9%)
  other arithmetic  28.9 us (9%)
  between operations  16.1 us (5%)
  Pallas kernels  9.8 us (3%)
    all_to_all x1, blocking collectives, exchanged(): return lax.all_to_all(pieces, axis, 0, 0, tiled=True)  31.7 us
    all_to_all x5, starting transfers between devices, exchanged(): return lax.all_to_all(pieces, axis, 0, 0, tiled=True)  28.7 us
    all_to_all x5, waiting for transfers between devices, exchanged(): return lax.all_to_all(pieces, axis, 0, 0, tiled=True)  28.5 us
    reduce_scatter x1, waiting for transfers between devices, step(): lax.psum_scatter(blocks.reshape(seq_size * rows_all, blocks.shape[2]), 's...  28.3 us
    dot_general x4, matrix products, contract_last(): lax.dot_general(left, right, (((1,), (1,)), ((), ())), preferred_element_...  16.6 us
    all_gather x1, blocking collectives, step(): token_grad = lax.all_gather(token_block, 'seq', axis=1, tiled=True)  16.2 us
    dot_general x5, matrix products, contract_first(): lax.dot_general(left, right, (((0,), (0,)), ((), ())), preferred_element_...  14.9 us
    all_gather x1, blocking collectives, step(): normed_grad = lax.all_gather(normed_mine, 'seq', axis=0, tiled=True)  14.6 us
  transfers between devices with their start and end apart: 16, of which 8 were waited for; matrix products, arithmetic and copies ran while one was open for 31% of the time, Pallas kernels for 0%

profile of v2, /device:TPU:1, one launch (start us, length us, event | category | flops | bytes accessed | tf_op | source)
XLA Modules:
  0.0 314.3 jit_solution(16807670198630345281)
XLA Ops:
  8.1 9.8 %column_blocks.1 = (bf16[1024,256]{1,0:T(8,128)(2,1)}, bf16[8,1024,640]{2,1,0:T(8,128)(2,1)}) custom-call(bf16[1024,256]{1,0:T(8,128)(2,1)} %hidden_ref.1, bf16[1024,256]{1,0:T(8,128)(2,1)} %gate_ref.1, bf16[5120,256]{1,0:T(8,128)(2,1)} %weight_ref.1), custom_call_target="tpu_custom_call" | custom-call | flops 2684354560 | bytes 14680064 | tf_op jit(solution)/shard_map/column_blocks/pallas_call | solution.py:82
  19.1 2.2 reshape.199
  22.5 3.8 %fusion.11 = bf16[16,96,320]{2,1,0:T(8,128)(2,1)} fusion(f32[96,16,320]{2,1,0:T(8,128)} %reshape.199, f32[16,320]{1,0:T(8,128)S(1)} %add.175, f32[16,320]{1,0:T(8,128)S(1)} %mul.187, f32[96,16]{0,1:T(8,128)S(1)} %bitcast.89, f32[96,16]{0,1:T(8,128)S(1)} %bitcast.90), kind=kLoop, calls=%fused_computation.37 | loop fusion | flops 2457600 | bytes 3002368 | tf_op jit(solution)/shard_map/transpose | solution.py:152
  26.3 8.6 %all-to-all-start = ((bf16[16,96,320]{2,1,0:T(8,128)(2,1)}), bf16[16,96,320]{2,1,0:T(8,128)(2,1)}, u32[]{:S(2)}, u32[]{:S(2)}) async-start(bf16[16,96,320]{2,1,0:T(8,128)(2,1)} %fusion.11), calls=%async_computation.1 | async-start | bytes 2359296 | tf_op jit(solution)/shard_map/all_to_all | solution.py:18
  35.0 1.8 reshape.198
  37.1 1.6 copy.59
  39.1 1.6 copy.58
  40.7 6.9 %multiply_convert_fusion.2 = (bf16[96,640]{1,0:T(8,128)(2,1)}, f32[96,640]{1,0:T(8,128)S(1)}) fusion(bf16[5120,640]{1,0:T(8,128)(2,1)} %param.25, f32[96,5120]{1,0:T(8,128)} %bitcast.78, f32[96,5120]{1,0:T(8,128)} %reshape.198, f32[96,5120]{1,0:T(8,128)} %bitcast.79, f32[5120]{0:T(1024)S(1)} %add.168, f32[5120]{0:T(1024)S(1)} %mul.170), kind=kOutput, calls=%fused_computation.66 | convolution fusion | flops 632279040 | bytes 12861440 | tf_op jit(solution)/shard_map/dot_general | solution.py:147
  49.6 3.1 fusion
  52.8 2.1 fusion.16
  54.8 28.3 %reduce-scatter.2.cloned.1.call-done = bf16[1024,640]{1,0:T(8,128)(2,1)} async-done(((bf16[8192,640]{1,0:T(8,128)(2,1)}), bf16[1024,640]{1,0:T(8,128)(2,1)}) %reduce-scatter.2.cloned.1.call-update) | async-done | bytes 1310736 | tf_op jit(solution)/shard_map/reduce_scatter | solution.py:135
  83.1 5.0 %convolution_convert_fusion.2 = bf16[1536,640]{1,0:T(8,128)(2,1)S(1)} fusion(bf16[1536,1024]{1,0:T(8,128)(2,1)} %fusion, bf16[1024,640]{1,0:T(8,128)(2,1)} %reduce-scatter.2.cloned.1.call-done), kind=kOutput, calls=%fused_computation.4 | convolution fusion | flops 2014248960 | bytes 6422528 | tf_op jit(solution)/shard_map/dot_general | solution.py:180
  88.1 31.7 %all_to_all.30 = bf16[16,96,640]{2,1,0:T(8,128)(2,1)} all-to-all(bf16[16,96,640]{2,1,0:T(8,128)(2,1)S(1)} %bitcast.85), channel_id=1, replica_groups=mesh['seq'=8,'span'=16] {'span'}, dimensions={0} | all-to-all | bytes 3932160 | tf_op jit(solution)/shard_map/all_to_all | solution.py:18
  119.8 1.8 reduce_sum.141
  121.6 16.2 %all_gather.16 = bf16[96,5120]{1,0:T(8,128)(2,1)S(1)} all-gather(bf16[96,640]{1,0:T(8,128)(2,1)S(1)} %reduce_sum.141), channel_id=1, replica_groups=mesh['seq'=8,'span'=16] {'seq'}, dimensions={1}, use_global_device_ids=true | all-gather | bytes 1105920 | tf_op jit(solution)/shard_map/all_gather | solution.py:184
  137.8 5.6 %fusion.12 = bf16[96,640]{1,0:T(8,128)(2,1)} fusion(f32[96,640]{1,0:T(8,128)S(1)} %get-tuple-element.48, bf16[96,5120]{1,0:T(8,128)(2,1)S(1)} %all_gather.16, bf16[640,5120]{1,0:T(8,128)(2,1)} %param.26), kind=kOutput, calls=%fused_computation.39 | convolution fusion | flops 629268480 | bytes 7905280 | tf_op jit(solution)/shard_map/dot_general | solution.py:58
  144.0 6.0 %convolution_convert_fusion.1 = bf16[96,5120]{1,0:T(8,128)(2,1)} fusion(bf16[96,640]{1,0:T(8,128)(2,1)} %fusion.12, bf16[5120,640]{1,0:T(8,128)(2,1)} %param.25), kind=kOutput, calls=%fused_computation.3 | convolution fusion | flops 629637120 | bytes 7659520 | tf_op jit(solution)/shard_map/dot_general | solution.py:58
  150.0 2.5 reshape.186
  152.5 4.3 %all-to-all-start.2 = ((bf16[8,48,1280]{2,1,0:T(8,128)(2,1)}), bf16[8,48,1280]{2,1,0:T(8,128)(2,1)}, u32[]{:S(2)}, u32[]{:S(2)}) async-start(bf16[8,48,1280]{2,1,0:T(8,128)(2,1)} %reshape.186), calls=%async_computation.3 | async-start | bytes 1966080 | tf_op jit(solution)/shard_map/all_to_all | solution.py:18
  156.8 1.8 reshape.187
  158.6 12.6 %all-to-all-done.2 = bf16[8,48,1280]{2,1,0:T(8,128)(2,1)} async-done(((bf16[8,48,1280]{2,1,0:T(8,128)(2,1)}), bf16[8,48,1280]{2,1,0:T(8,128)(2,1)}, u32[]{:S(2)}, u32[]{:S(2)}) %all-to-all-start.2) | async-done | bytes 983072 | tf_op jit(solution)/shard_map/all_to_all | solution.py:18
  172.5 2.6 copy.54
  175.1 4.4 %all-to-all-start.3 = ((bf16[16,96,320]{2,1,0:T(8,128)(2,1)}), bf16[16,96,320]{2,1,0:T(8,128)(2,1)}, u32[]{:S(2)}, u32[]{:S(2)}) async-start(bf16[16,96,320]{2,1,0:T(8,128)(2,1)} %copy.54), calls=%async_computation.4 | async-start | bytes 2359296 | tf_op jit(solution)/shard_map/all_to_all | solution.py:18
  179.5 14.6 %all_gather.17 = bf16[384,1280]{1,0:T(8,128)(2,1)S(1)} all-gather(bf16[48,1280]{1,0:T(8,128)(2,1)S(1)} %reduce_sum.142), channel_id=1, replica_groups=mesh['seq'=8,'span'=16] {'seq'}, dimensions={0}, use_global_device_ids=true | all-gather | bytes 1105920 | tf_op jit(solution)/shard_map/all_gather | solution.py:201
  194.1 2.0 fusion.7
  197.5 2.2 convolution_convert_fusion.4
  199.8 3.0 fusion.10
  202.8 2.2 fusion.1
  205.1 7.0 %all-to-all-start.4 = ((bf16[16,40,1280]{2,1,0:T(8,128)(2,1)}), bf16[16,40,1280]{2,1,0:T(8,128)(2,1)}, u32[]{:S(2)}, u32[]{:S(2)}) async-start(bf16[16,40,1280]{2,1,0:T(8,128)(2,1)} %bitcast.82), calls=%async_computation.5 | async-start | bytes 3276800 | tf_op jit(solution)/shard_map/all_to_all | solution.py:18
  212.1 1.9 convolution_convert_fusion.5
  214.0 2.3 convolution_convert_fusion.6
  220.3 1.9 fusion.6
  222.2 2.9 copy.55
  225.1 2.8 pad_maximum_fusion
  227.9 8.9 %all-to-all-done.4 = bf16[16,40,1280]{2,1,0:T(8,128)(2,1)} async-done(((bf16[16,40,1280]{2,1,0:T(8,128)(2,1)}), bf16[16,40,1280]{2,1,0:T(8,128)(2,1)}, u32[]{:S(2)}, u32[]{:S(2)}) %all-to-all-start.4) | async-done | bytes 1638432 | tf_op jit(solution)/shard_map/all_to_all | solution.py:18
  236.7 4.5 %all-to-all-start.5 = ((bf16[16,114,640]{2,1,0:T(8,128)(2,1)}), bf16[16,114,640]{2,1,0:T(8,128)(2,1)}, u32[]{:S(2)}, u32[]{:S(2)}) async-start(bf16[16,114,640]{2,1,0:T(8,128)(2,1)} %pad_maximum_fusion), calls=%async_computation.6 | async-start | bytes 4915200 | tf_op jit(solution)/shard_map/all_to_all | solution.py:18
  242.1 1.6 collective-permute-start
  247.7 2.6 collective-permute-start.4
  250.3 3.0 collective-permute-done.1
  253.3 1.6 dynamic-slice_bitcast_fusion.7
  254.9 4.3 %collective-permute-done.2 = bf16[48,1280]{1,0:T(8,128)(2,1)S(1)} collective-permute-done((bf16[48,1280]{1,0:T(8,128)(2,1)S(1)}, bf16[48,1280]{1,0:T(8,128)(2,1)S(1)}, u32[]{:S(2)}, u32[]{:S(2)}) %collective-permute-start.2) | collective-permute-done | bytes 122912 | tf_op jit(solution)/shard_map/ppermute | solution.py:34
  260.6 2.3 reduce_sum.150
  262.9 3.6 %convolution_convert_fusion.7 = bf16[320,640]{1,0:T(8,128)(2,1)} fusion(bf16[1536,320]{1,0:T(8,128)(2,1)} %bitcast.6, bf16[1536,640]{1,0:T(8,128)(2,1)} %all-gather.8.cloned.1.call-done), kind=kOutput, calls=%fused_computation.36 | convolution fusion | flops 629350400 | bytes 3358720 | tf_op jit(solution)/shard_map/dot_general | solution.py:64
  266.6 7.0 %all-to-all-done.5 = bf16[16,114,640]{2,1,0:T(8,128)(2,1)} async-done(((bf16[16,114,640]{2,1,0:T(8,128)(2,1)}), bf16[16,114,640]{2,1,0:T(8,128)(2,1)}, u32[]{:S(2)}, u32[]{:S(2)}) %all-to-all-start.5) | async-done | bytes 2334752 | tf_op jit(solution)/shard_map/all_to_all | solution.py:18
  279.8 2.4 slice_reduce_fusion
  282.2 11.5 %all-gather.4.cloned.1.call-done = bf16[1024,5120]{1,0:T(8,128)(2,1)} async-done(((bf16[8,5120]{1,0:T(8,128)(2,1)}), bf16[1024,5120]{1,0:T(8,128)(2,1)}) %all-gather.4.cloned.1.call-update) | async-done | bytes 10485776 | tf_op jit(solution)/shard_map/all_gather | solution.py:183
  293.7 8.5 %fusion.9 = bf16[1024,256]{1,0:T(8,128)(2,1)} fusion(bf16[1024,5120]{1,0:T(8,128)(2,1)} %all-gather.4.cloned.1.call-done, bf16[5120,256]{1,0:T(8,128)(2,1)} %weight_ref.1, bf16[1024,256]{1,0:T(8,128)(2,1)S(1)} %copy-done.14), kind=kOutput, calls=%fused_computation.33 | convolution fusion | flops 2685140992 | bytes 14155776 | tf_op jit(solution)/shard_map/dot_general | solution.py:194
  302.3 4.5 %convolution_convert_fusion = bf16[5120,256]{1,0:T(8,128)(2,1)} fusion(bf16[1024,5120]{1,0:T(8,128)(2,1)S(1)} %copy-done.12, bf16[1024,256]{1,0:T(8,128)(2,1)S(1)} %copy-done.16), kind=kOutput, calls=%fused_computation | convolution fusion | flops 2685665280 | bytes 13631488 | tf_op jit(solution)/shard_map/dot_general | solution.py:64
  (111 shorter events, 25.0 us)
Async XLA Ops:
  8.0 44.7 %copy-start = (bf16[1280,640]{1,0:T(8,128)(2,1)S(1)}, bf16[1280,640]{1,0:T(8,128)(2,1)}, u32[]{:S(2)}) copy-start(bf16[1280,640]{1,0:T(8,128)(2,1)} %param.27) | copy-start | bytes 4915204
  8.0 75.1 %reduce-scatter.2.cloned.1.call-start = ((), (), s32[]{:S(2)}) async-start(), calls=%async_computation.7 | async-start | bytes 11796480 | tf_op jit(solution)/shard_map/reduce_scatter | solution.py:135
  17.9 1.2 copy-start.2
  19.1 3.2 %copy-start.9 = (f32[1280]{0:T(1024)S(1)}, f32[1280]{0:T(1024)}, u32[]{:S(2)}) copy-start(f32[1280]{0:T(1024)} %param.24) | copy-start | bytes 15364
  21.2 1.1 copy-start.8
  26.3 28.5 %all-to-all-start = ((bf16[16,96,320]{2,1,0:T(8,128)(2,1)}), bf16[16,96,320]{2,1,0:T(8,128)(2,1)}, u32[]{:S(2)}, u32[]{:S(2)}) async-start(bf16[16,96,320]{2,1,0:T(8,128)(2,1)} %fusion.11), calls=%async_computation.1 | async-start | bytes 2359296 | tf_op jit(solution)/shard_map/all_to_all | solution.py:18
  35.0 170.1 %all-gather.6.cloned.1.call-start = ((), (), s32[]{:S(2)}) async-start(), calls=%async_computation.9 | async-start | bytes 2088960 | tf_op jit(solution)/shard_map/all_gather | solution.py:150
  47.6 1.6 copy-start.11
  47.6 2.0 copy-start.10
  47.7 215.3 %all-gather.8.cloned.1.call-start = ((), (), s32[]{:S(2)}) async-start(), calls=%async_computation.10 | async-start | bytes 2088960 | tf_op jit(solution)/shard_map/all_gather | solution.py:187
  49.3 3.5 %copy-start.5 = (bf16[1,384,1280]{2,1,0:T(8,128)(2,1)S(1)}, bf16[1,384,1280]{2,1,0:T(8,128)(2,1)}, u32[]{:S(2)}) copy-start(bf16[1,384,1280]{2,1,0:T(8,128)(2,1)} %param.22) | copy-start | bytes 2949124
  49.3 3.5 %copy-start.15 = (f32[640]{0:T(1024)S(1)}, f32[640]{0:T(1024)}, u32[]{:S(2)}) copy-start(f32[640]{0:T(1024)} %param.28) | copy-start | bytes 7684
  143.4 150.3 %all-gather.4.cloned.1.call-start = ((), (), s32[]{:S(2)}) async-start(), calls=%async_computation.8 | async-start | bytes 10567680 | tf_op jit(solution)/shard_map/all_gather | solution.py:183
  152.5 18.7 %all-to-all-start.2 = ((bf16[8,48,1280]{2,1,0:T(8,128)(2,1)}), bf16[8,48,1280]{2,1,0:T(8,128)(2,1)}, u32[]{:S(2)}, u32[]{:S(2)}) async-start(bf16[8,48,1280]{2,1,0:T(8,128)(2,1)} %reshape.186), calls=%async_computation.3 | async-start | bytes 1966080 | tf_op jit(solution)/shard_map/all_to_all | solution.py:18
  175.1 24.7 %all-to-all-start.3 = ((bf16[16,96,320]{2,1,0:T(8,128)(2,1)}), bf16[16,96,320]{2,1,0:T(8,128)(2,1)}, u32[]{:S(2)}, u32[]{:S(2)}) async-start(bf16[16,96,320]{2,1,0:T(8,128)(2,1)} %copy.54), calls=%async_computation.4 | async-start | bytes 2359296 | tf_op jit(solution)/shard_map/all_to_all | solution.py:18
  179.5 16.6 %copy-start.1 = (f32[384,1280]{1,0:T(8,128)S(1)}, f32[384,1280]{1,0:T(8,128)}, u32[]{:S(2)}) copy-start(f32[384,1280]{1,0:T(8,128)} %fusion.8) | copy-start | bytes 5898244
  196.6 1.0 copy-start.3
  199.8 3.0 copy-start.6
  202.8 9.2 %copy-start.4 = (bf16[384,640]{1,0:T(8,128)(2,1)}, bf16[384,640]{1,0:T(8,128)(2,1)S(1)}, u32[]{:S(2)}) copy-start(bf16[384,640]{1,0:T(8,128)(2,1)S(1)} %fusion.10) | copy-start | bytes 1474564
  205.1 31.7 %all-to-all-start.4 = ((bf16[16,40,1280]{2,1,0:T(8,128)(2,1)}), bf16[16,40,1280]{2,1,0:T(8,128)(2,1)}, u32[]{:S(2)}, u32[]{:S(2)}) async-start(bf16[16,40,1280]{2,1,0:T(8,128)(2,1)} %bitcast.82), calls=%async_computation.5 | async-start | bytes 3276800 | tf_op jit(solution)/shard_map/all_to_all | solution.py:18
  212.1 1.9 copy-start.13
  227.9 13.5 %copy-start.7 = (bf16[384,1280]{1,0:T(8,128)(2,1)S(1)}, bf16[384,1280]{1,0:T(8,128)(2,1)}, u32[]{:S(2)}) copy-start(bf16[384,1280]{1,0:T(8,128)(2,1)} %convolution_convert_fusion.5) | copy-start | bytes 2949124
  236.7 36.8 %all-to-all-start.5 = ((bf16[16,114,640]{2,1,0:T(8,128)(2,1)}), bf16[16,114,640]{2,1,0:T(8,128)(2,1)}, u32[]{:S(2)}, u32[]{:S(2)}) async-start(bf16[16,114,640]{2,1,0:T(8,128)(2,1)} %pad_maximum_fusion), calls=%async_computation.6 | async-start | bytes 4915200 | tf_op jit(solution)/shard_map/all_to_all | solution.py:18
  242.1 8.2 %collective-permute-start = (bf16[48,1280]{1,0:T(8,128)(2,1)}, bf16[48,1280]{1,0:T(8,128)(2,1)S(1)}, u32[]{:S(2)}, u32[]{:S(2)}) collective-permute-start(bf16[48,1280]{1,0:T(8,128)(2,1)} %get-tuple-element.72), channel_id=1, source_target_pairs={{0,16},{16,32},{32,48},{48,64},{64,80},{80,96},{96,112},{112,0},{1... | collective-permute-start | bytes 368648 | tf_op jit(solution)/shard_map/ppermute | solution.py:34
  243.7 9.6 %collective-permute-start.1 = (bf16[48,1280]{1,0:T(8,128)(2,1)}, bf16[48,1280]{1,0:T(8,128)(2,1)S(1)}, u32[]{:S(2)}, u32[]{:S(2)}) collective-permute-start(bf16[48,1280]{1,0:T(8,128)(2,1)} %get-tuple-element.78), channel_id=1, source_target_pairs={{0,32},{16,48},{32,64},{48,80},{64,96},{80,112},{96,0},{112,16},{1... | collective-permute-start | bytes 368648 | tf_op jit(solution)/shard_map/ppermute | solution.py:34
  244.8 14.4 %collective-permute-start.2 = (bf16[48,1280]{1,0:T(8,128)(2,1)S(1)}, bf16[48,1280]{1,0:T(8,128)(2,1)S(1)}, u32[]{:S(2)}, u32[]{:S(2)}) collective-permute-start(bf16[48,1280]{1,0:T(8,128)(2,1)S(1)} %get-tuple-element.77), channel_id=1, source_target_pairs={{0,48},{16,64},{32,80},{48,96},{64,112},{80,0},{96,16},{112,32},{1... | collective-permute-start | bytes 368648 | tf_op jit(solution)/shard_map/ppermute | solution.py:34
  246.3 12.9 %collective-permute-start.3 = (bf16[48,1280]{1,0:T(8,128)(2,1)S(1)}, bf16[48,1280]{1,0:T(8,128)(2,1)S(1)}, u32[]{:S(2)}, u32[]{:S(2)}) collective-permute-start(bf16[48,1280]{1,0:T(8,128)(2,1)S(1)} %get-tuple-element.76), channel_id=1, source_target_pairs={{0,64},{16,80},{32,96},{48,112},{64,0},{80,16},{96,32},{112,48},{1... | collective-permute-start | bytes 368648 | tf_op jit(solution)/shard_map/ppermute | solution.py:34
  247.7 11.5 %collective-permute-start.4 = (bf16[48,1280]{1,0:T(8,128)(2,1)S(1)}, bf16[48,1280]{1,0:T(8,128)(2,1)S(1)}, u32[]{:S(2)}, u32[]{:S(2)}) collective-permute-start(bf16[48,1280]{1,0:T(8,128)(2,1)S(1)} %get-tuple-element.75), channel_id=1, source_target_pairs={{0,80},{16,96},{32,112},{48,0},{64,16},{80,32},{96,48},{112,64},{1... | collective-permute-start | bytes 368648 | tf_op jit(solution)/shard_map/ppermute | solution.py:34
  250.3 8.9 %collective-permute-start.5 = (bf16[48,1280]{1,0:T(8,128)(2,1)S(1)}, bf16[48,1280]{1,0:T(8,128)(2,1)S(1)}, u32[]{:S(2)}, u32[]{:S(2)}) collective-permute-start(bf16[48,1280]{1,0:T(8,128)(2,1)S(1)} %get-tuple-element.74), channel_id=1, source_target_pairs={{0,96},{16,112},{32,0},{48,16},{64,32},{80,48},{96,64},{112,80},{1... | collective-permute-start | bytes 368648 | tf_op jit(solution)/shard_map/ppermute | solution.py:34
  253.3 6.5 %collective-permute-start.6 = (bf16[48,1280]{1,0:T(8,128)(2,1)S(1)}, bf16[48,1280]{1,0:T(8,128)(2,1)S(1)}, u32[]{:S(2)}, u32[]{:S(2)}) collective-permute-start(bf16[48,1280]{1,0:T(8,128)(2,1)S(1)} %get-tuple-element.73), channel_id=1, source_target_pairs={{0,112},{16,0},{32,16},{48,32},{64,48},{80,64},{96,80},{112,96},{1... | collective-permute-start | bytes 368648 | tf_op jit(solution)/shard_map/ppermute | solution.py:34
  275.0 18.8 %copy-start.14 = (bf16[1024,256]{1,0:T(8,128)(2,1)S(1)}, bf16[1024,256]{1,0:T(8,128)(2,1)}, u32[]{:S(2)}) copy-start(bf16[1024,256]{1,0:T(8,128)(2,1)} %hidden_ref.1) | copy-start | bytes 1572868
  282.2 20.0 %copy-start.16 = (bf16[1024,256]{1,0:T(8,128)(2,1)S(1)}, bf16[1024,256]{1,0:T(8,128)(2,1)}, u32[]{:S(2)}) copy-start(bf16[1024,256]{1,0:T(8,128)(2,1)} %get-tuple-element.44) | copy-start | bytes 1572868
  293.7 8.5 %copy-start.12 = (bf16[1024,5120]{1,0:T(8,128)(2,1)S(1)}, bf16[1024,5120]{1,0:T(8,128)(2,1)}, u32[]{:S(2)}) copy-start(bf16[1024,5120]{1,0:T(8,128)(2,1)} %all-gather.4.cloned.1.call-done) | copy-start | bytes 31457284
Sparse Core Ops, SparseCore 0:
  18.0 65.0 reduce-scatter.1
Sparse Core Ops, SparseCore 1:
  47.7 45.1 all-gather.5
  143.5 39.6 all-gather.7
  186.0 107.7 all-gather.3

commit v3 on v2

--- a/solution.py
+++ b/solution.py
@@ -3,6 +3,7 @@
 import jax
 import jax.numpy as jnp
 from jax import lax
+from jax.experimental.layout import Layout, with_layout_constraint
 from jax.experimental import pallas as pl
 from jax.sharding import PartitionSpec as P
 
@@ -189,7 +190,9 @@
     normed_part, token_grad = lax.optimization_barrier((normed_part, token_grad))
     normed_pieces = exchanged(normed_part.reshape(seq_size, mine_frames, width), "seq")
 
-    token_cols = jnp.moveaxis(token_grad.reshape(slots_each, owner_count, -1), 1, 0)
+    token_cols = with_layout_constraint(
+        jnp.moveaxis(token_grad.reshape(slots_each, owner_count, -1), 1, 0), Layout((0, 1, 2))
+    )
 
     up_rows = jnp.dot(piece, up_weight, preferred_element_type=jnp.float32)
     gate_act_grad = (hidden_grad.astype(jnp.float32) * up_rows).astype(jnp.bfloat16)

time: 316 us -> 326 us (1.032)
  waiting for transfers between devices: 76.8 us -> 87.1 us
    all_gather x1, waiting for transfers between devices: 11.5 us -> 20.1 us  [step(): piece = lax.all_gather(llm_input, ('seq', 'span'), axis=0, tiled=True)]
  transfers between devices with their start and end apart: 16 -> 16, of which waited for: 8 -> 8; matrix products, arithmetic and copies ran while one was open for 31% -> 30% of each run, Pallas kernels for 0% -> 0%
where the time goes in v3:
time: 326 us; the launch traced here: 324 us
  waiting for transfers between devices  87.1 us (27%)
  blocking collectives  62.5 us (19%)
  matrix products  53.9 us (17%)
  starting transfers between devices  37.1 us (11%)
  local copies, waits for them, and re-layouts  29.2 us (9%)
  other arithmetic  28.8 us (9%)
  between operations  16.1 us (5%)
  Pallas kernels  9.8 us (3%)
    all_to_all x1, blocking collectives, exchanged(): return lax.all_to_all(pieces, axis, 0, 0, tiled=True)  31.7 us
    all_to_all x5, waiting for transfers between devices, exchanged(): return lax.all_to_all(pieces, axis, 0, 0, tiled=True)  29.6 us
    all_to_all x5, starting transfers between devices, exchanged(): return lax.all_to_all(pieces, axis, 0, 0, tiled=True)  28.7 us
    reduce_scatter x1, waiting for transfers between devices, step(): lax.psum_scatter(blocks.reshape(seq_size * rows_all, blocks.shape[2]), 's...  28.3 us
    all_gather x1, waiting for transfers between devices, step(): piece = lax.all_gather(llm_input, ('seq', 'span'), axis=0, tiled=True)  20.1 us
    dot_general x4, matrix products, contract_last(): lax.dot_general(left, right, (((1,), (1,)), ((), ())), preferred_element_...  16.6 us
    all_gather x1, blocking collectives, step(): token_grad = lax.all_gather(token_block, 'seq', axis=1, tiled=True)  16.2 us
    dot_general x5, matrix products, contract_first(): lax.dot_general(left, right, (((0,), (0,)), ((), ())), preferred_element_...  14.9 us
  transfers between devices with their start and end apart: 16, of which 8 were waited for; matrix products, arithmetic and copies ran while one was open for 30% of the time, Pallas kernels for 0%

profile of v3, /device:TPU:1, one launch (start us, length us, event | category | flops | bytes accessed | tf_op | source)
XLA Modules:
  0.0 324.4 jit_solution(14023138960753748656)
XLA Ops:
  8.1 9.8 %column_blocks.1 = (bf16[1024,256]{1,0:T(8,128)(2,1)}, bf16[8,1024,640]{2,1,0:T(8,128)(2,1)}) custom-call(bf16[1024,256]{1,0:T(8,128)(2,1)} %hidden_ref.1, bf16[1024,256]{1,0:T(8,128)(2,1)} %gate_ref.1, bf16[5120,256]{1,0:T(8,128)(2,1)} %weight_ref.1), custom_call_target="tpu_custom_call" | custom-call | flops 2684354560 | bytes 14680064 | tf_op jit(solution)/shard_map/column_blocks/pallas_call | solution.py:83
  19.1 2.2 reshape.199
  22.5 3.8 %fusion.11 = bf16[16,96,320]{2,1,0:T(8,128)(2,1)} fusion(f32[96,16,320]{2,1,0:T(8,128)} %reshape.199, f32[16,320]{1,0:T(8,128)S(1)} %add.175, f32[16,320]{1,0:T(8,128)S(1)} %mul.187, f32[96,16]{0,1:T(8,128)S(1)} %bitcast.90, f32[96,16]{0,1:T(8,128)S(1)} %bitcast.91), kind=kLoop, calls=%fused_computation.37 | loop fusion | flops 2457600 | bytes 3002368 | tf_op jit(solution)/shard_map/transpose | solution.py:153
  26.3 8.6 %all-to-all-start = ((bf16[16,96,320]{2,1,0:T(8,128)(2,1)}), bf16[16,96,320]{2,1,0:T(8,128)(2,1)}, u32[]{:S(2)}, u32[]{:S(2)}) async-start(bf16[16,96,320]{2,1,0:T(8,128)(2,1)} %fusion.11), calls=%async_computation.1 | async-start | bytes 2359296 | tf_op jit(solution)/shard_map/all_to_all | solution.py:19
  35.0 1.8 reshape.198
  37.1 1.6 copy.52
  39.1 1.6 copy.51
  40.7 6.9 %multiply_convert_fusion.2 = (bf16[96,640]{1,0:T(8,128)(2,1)}, f32[96,640]{1,0:T(8,128)S(1)}) fusion(bf16[5120,640]{1,0:T(8,128)(2,1)} %param.25, f32[96,5120]{1,0:T(8,128)} %bitcast.80, f32[96,5120]{1,0:T(8,128)} %reshape.198, f32[96,5120]{1,0:T(8,128)} %bitcast.81, f32[5120]{0:T(1024)S(1)} %add.168, f32[5120]{0:T(1024)S(1)} %mul.170), kind=kOutput, calls=%fused_computation.67 | convolution fusion | flops 632279040 | bytes 12861440 | tf_op jit(solution)/shard_map/dot_general | solution.py:148
  47.7 1.6 fusion.8
  49.6 3.1 fusion
  52.8 2.1 fusion.16
  54.8 28.3 %reduce-scatter.2.cloned.1.call-done = bf16[1024,640]{1,0:T(8,128)(2,1)} async-done(((bf16[8192,640]{1,0:T(8,128)(2,1)}), bf16[1024,640]{1,0:T(8,128)(2,1)}) %reduce-scatter.2.cloned.1.call-update) | async-done | bytes 1310736 | tf_op jit(solution)/shard_map/reduce_scatter | solution.py:136
  83.1 5.0 %convolution_convert_fusion.2 = bf16[1536,640]{1,0:T(8,128)(2,1)S(1)} fusion(bf16[1536,1024]{1,0:T(8,128)(2,1)} %fusion, bf16[1024,640]{1,0:T(8,128)(2,1)} %reduce-scatter.2.cloned.1.call-done), kind=kOutput, calls=%fused_computation.4 | convolution fusion | flops 2014248960 | bytes 6422528 | tf_op jit(solution)/shard_map/dot_general | solution.py:181
  88.1 31.7 %all_to_all.30 = bf16[16,96,640]{2,1,0:T(8,128)(2,1)} all-to-all(bf16[16,96,640]{2,1,0:T(8,128)(2,1)S(1)} %bitcast.86), channel_id=1, replica_groups=mesh['seq'=8,'span'=16] {'span'}, dimensions={0} | all-to-all | bytes 3932160 | tf_op jit(solution)/shard_map/all_to_all | solution.py:19
  119.8 1.8 reduce_sum.141
  121.6 16.2 %all_gather.16 = bf16[96,5120]{1,0:T(8,128)(2,1)S(1)} all-gather(bf16[96,640]{1,0:T(8,128)(2,1)S(1)} %reduce_sum.141), channel_id=1, replica_groups=mesh['seq'=8,'span'=16] {'seq'}, dimensions={1}, use_global_device_ids=true | all-gather | bytes 1105920 | tf_op jit(solution)/shard_map/all_gather | solution.py:185
  137.8 5.6 %fusion.12 = bf16[96,640]{1,0:T(8,128)(2,1)} fusion(f32[96,640]{1,0:T(8,128)S(1)} %get-tuple-element.48, bf16[96,5120]{1,0:T(8,128)(2,1)S(1)} %all_gather.16, bf16[640,5120]{1,0:T(8,128)(2,1)} %param.26), kind=kOutput, calls=%fused_computation.40 | convolution fusion | flops 629268480 | bytes 7905280 | tf_op jit(solution)/shard_map/dot_general | solution.py:59
  144.0 6.0 %convolution_convert_fusion.1 = bf16[96,5120]{1,0:T(8,128)(2,1)} fusion(bf16[96,640]{1,0:T(8,128)(2,1)} %fusion.12, bf16[5120,640]{1,0:T(8,128)(2,1)} %param.25), kind=kOutput, calls=%fused_computation.3 | convolution fusion | flops 629637120 | bytes 7659520 | tf_op jit(solution)/shard_map/dot_general | solution.py:59
  150.0 2.5 reshape.186
  152.5 4.3 %all-to-all-start.2 = ((bf16[8,48,1280]{2,1,0:T(8,128)(2,1)}), bf16[8,48,1280]{2,1,0:T(8,128)(2,1)}, u32[]{:S(2)}, u32[]{:S(2)}) async-start(bf16[8,48,1280]{2,1,0:T(8,128)(2,1)} %reshape.186), calls=%async_computation.3 | async-start | bytes 1966080 | tf_op jit(solution)/shard_map/all_to_all | solution.py:19
  156.8 1.8 reshape.187
  158.6 2.6 copy.65
  161.2 10.1 %all-to-all-done.2 = bf16[8,48,1280]{2,1,0:T(8,128)(2,1)} async-done(((bf16[8,48,1280]{2,1,0:T(8,128)(2,1)}), bf16[8,48,1280]{2,1,0:T(8,128)(2,1)}, u32[]{:S(2)}, u32[]{:S(2)}) %all-to-all-start.2) | async-done | bytes 983072 | tf_op jit(solution)/shard_map/all_to_all | solution.py:19
  172.6 4.4 %all-to-all-start.3 = ((bf16[16,96,320]{2,1,0:T(8,128)(2,1)}), bf16[16,96,320]{2,1,0:T(8,128)(2,1)}, u32[]{:S(2)}, u32[]{:S(2)}) async-start(bf16[16,96,320]{2,1,0:T(8,128)(2,1)} %bitcast.78), calls=%async_computation.4 | async-start | bytes 2359296 | tf_op jit(solution)/shard_map/all_to_all | solution.py:19
  177.0 14.6 %all_gather.17 = bf16[384,1280]{1,0:T(8,128)(2,1)S(1)} all-gather(bf16[48,1280]{1,0:T(8,128)(2,1)S(1)} %reduce_sum.142), channel_id=1, replica_groups=mesh['seq'=8,'span'=16] {'seq'}, dimensions={0}, use_global_device_ids=true | all-gather | bytes 1105920 | tf_op jit(solution)/shard_map/all_gather | solution.py:204
  191.6 2.0 fusion.7
  195.0 2.2 convolution_convert_fusion.4
  197.2 3.0 fusion.10
  200.3 2.2 fusion.1
  202.5 6.9 %all-to-all-start.4 = ((bf16[16,40,1280]{2,1,0:T(8,128)(2,1)}), bf16[16,40,1280]{2,1,0:T(8,128)(2,1)}, u32[]{:S(2)}, u32[]{:S(2)}) async-start(bf16[16,40,1280]{2,1,0:T(8,128)(2,1)} %bitcast.84), calls=%async_computation.5 | async-start | bytes 3276800 | tf_op jit(solution)/shard_map/all_to_all | solution.py:19
  209.5 1.9 convolution_convert_fusion.5
  211.4 2.3 convolution_convert_fusion.6
  217.7 1.9 fusion.6
  219.6 2.9 copy.48
  222.6 2.8 pad_maximum_fusion
  225.3 9.0 %all-to-all-done.4 = bf16[16,40,1280]{2,1,0:T(8,128)(2,1)} async-done(((bf16[16,40,1280]{2,1,0:T(8,128)(2,1)}), bf16[16,40,1280]{2,1,0:T(8,128)(2,1)}, u32[]{:S(2)}, u32[]{:S(2)}) %all-to-all-start.4) | async-done | bytes 1638432 | tf_op jit(solution)/shard_map/all_to_all | solution.py:19
  234.3 4.5 %all-to-all-start.5 = ((bf16[16,114,640]{2,1,0:T(8,128)(2,1)}), bf16[16,114,640]{2,1,0:T(8,128)(2,1)}, u32[]{:S(2)}, u32[]{:S(2)}) async-start(bf16[16,114,640]{2,1,0:T(8,128)(2,1)} %pad_maximum_fusion), calls=%async_computation.6 | async-start | bytes 4915200 | tf_op jit(solution)/shard_map/all_to_all | solution.py:19
  245.2 2.6 collective-permute-start.4
  247.9 3.9 %collective-permute-done.1 = bf16[48,1280]{1,0:T(8,128)(2,1)S(1)} collective-permute-done((bf16[48,1280]{1,0:T(8,128)(2,1)}, bf16[48,1280]{1,0:T(8,128)(2,1)S(1)}, u32[]{:S(2)}, u32[]{:S(2)}) %collective-permute-start.1) | collective-permute-done | bytes 122912 | tf_op jit(solution)/shard_map/ppermute | solution.py:35
  251.8 1.6 dynamic-slice_bitcast_fusion.7
  253.3 4.0 %collective-permute-done.2 = bf16[48,1280]{1,0:T(8,128)(2,1)S(1)} collective-permute-done((bf16[48,1280]{1,0:T(8,128)(2,1)S(1)}, bf16[48,1280]{1,0:T(8,128)(2,1)S(1)}, u32[]{:S(2)}, u32[]{:S(2)}) %collective-permute-start.2) | collective-permute-done | bytes 122912 | tf_op jit(solution)/shard_map/ppermute | solution.py:35
  258.7 2.3 reduce_sum.150
  261.0 3.6 %convolution_convert_fusion.7 = bf16[320,640]{1,0:T(8,128)(2,1)} fusion(bf16[1536,320]{1,0:T(8,128)(2,1)} %bitcast.6, bf16[1536,640]{1,0:T(8,128)(2,1)} %all-gather.8.cloned.1.call-done), kind=kOutput, calls=%fused_computation.36 | convolution fusion | flops 629350400 | bytes 3358720 | tf_op jit(solution)/shard_map/dot_general | solution.py:65
  264.7 10.5 %all-to-all-done.5 = bf16[16,114,640]{2,1,0:T(8,128)(2,1)} async-done(((bf16[16,114,640]{2,1,0:T(8,128)(2,1)}), bf16[16,114,640]{2,1,0:T(8,128)(2,1)}, u32[]{:S(2)}, u32[]{:S(2)}) %all-to-all-start.5) | async-done | bytes 2334752 | tf_op jit(solution)/shard_map/all_to_all | solution.py:19
  281.4 2.3 slice_reduce_fusion
  283.8 20.1 %all-gather.4.cloned.1.call-done = bf16[1024,5120]{1,0:T(8,128)(2,1)} async-done(((bf16[8,5120]{1,0:T(8,128)(2,1)}), bf16[1024,5120]{1,0:T(8,128)(2,1)}) %all-gather.4.cloned.1.call-update) | async-done | bytes 10485776 | tf_op jit(solution)/shard_map/all_gather | solution.py:184
  303.8 8.5 %fusion.9 = bf16[1024,256]{1,0:T(8,128)(2,1)} fusion(bf16[1024,5120]{1,0:T(8,128)(2,1)} %all-gather.4.cloned.1.call-done, bf16[5120,256]{1,0:T(8,128)(2,1)} %weight_ref.1, bf16[1024,256]{1,0:T(8,128)(2,1)S(1)} %copy-done.14), kind=kOutput, calls=%fused_computation.33 | convolution fusion | flops 2685140992 | bytes 14155776 | tf_op jit(solution)/shard_map/dot_general | solution.py:197
  312.4 4.5 %convolution_convert_fusion = bf16[5120,256]{1,0:T(8,128)(2,1)} fusion(bf16[1024,5120]{1,0:T(8,128)(2,1)S(1)} %copy-done.12, bf16[1024,256]{1,0:T(8,128)(2,1)S(1)} %copy-done.16), kind=kOutput, calls=%fused_computation | convolution fusion | flops 2685665280 | bytes 13631488 | tf_op jit(solution)/shard_map/dot_general | solution.py:65
  (111 shorter events, 25.0 us)
Async XLA Ops:
  8.0 44.7 %copy-start = (bf16[1280,640]{1,0:T(8,128)(2,1)S(1)}, bf16[1280,640]{1,0:T(8,128)(2,1)}, u32[]{:S(2)}) copy-start(bf16[1280,640]{1,0:T(8,128)(2,1)} %param.27) | copy-start | bytes 4915204
  8.0 75.1 %reduce-scatter.2.cloned.1.call-start = ((), (), s32[]{:S(2)}) async-start(), calls=%async_computation.7 | async-start | bytes 11796480 | tf_op jit(solution)/shard_map/reduce_scatter | solution.py:136
  17.9 1.2 copy-start.2
  19.1 3.2 copy-start.9
  21.2 1.1 copy-start.8
  26.3 28.5 %all-to-all-start = ((bf16[16,96,320]{2,1,0:T(8,128)(2,1)}), bf16[16,96,320]{2,1,0:T(8,128)(2,1)}, u32[]{:S(2)}, u32[]{:S(2)}) async-start(bf16[16,96,320]{2,1,0:T(8,128)(2,1)} %fusion.11), calls=%async_computation.1 | async-start | bytes 2359296 | tf_op jit(solution)/shard_map/all_to_all | solution.py:19
  35.0 167.6 %all-gather.6.cloned.1.call-start = ((), (), s32[]{:S(2)}) async-start(), calls=%async_computation.9 | async-start | bytes 2088960 | tf_op jit(solution)/shard_map/all_gather | solution.py:151
  47.6 1.6 copy-start.11
  47.6 2.0 copy-start.10
  47.7 213.4 %all-gather.8.cloned.1.call-start = ((), (), s32[]{:S(2)}) async-start(), calls=%async_computation.10 | async-start | bytes 2088960 | tf_op jit(solution)/shard_map/all_gather | solution.py:188
  49.3 3.5 %copy-start.5 = (bf16[1,384,1280]{2,1,0:T(8,128)(2,1)S(1)}, bf16[1,384,1280]{2,1,0:T(8,128)(2,1)}, u32[]{:S(2)}) copy-start(bf16[1,384,1280]{2,1,0:T(8,128)(2,1)} %param.22) | copy-start | bytes 2949124
  49.3 3.5 %copy-start.15 = (f32[640]{0:T(1024)S(1)}, f32[640]{0:T(1024)}, u32[]{:S(2)}) copy-start(f32[640]{0:T(1024)} %param.28) | copy-start | bytes 7684
  143.4 160.4 %all-gather.4.cloned.1.call-start = ((), (), s32[]{:S(2)}) async-start(), calls=%async_computation.8 | async-start | bytes 10567680 | tf_op jit(solution)/shard_map/all_gather | solution.py:184
  152.5 18.7 %all-to-all-start.2 = ((bf16[8,48,1280]{2,1,0:T(8,128)(2,1)}), bf16[8,48,1280]{2,1,0:T(8,128)(2,1)}, u32[]{:S(2)}, u32[]{:S(2)}) async-start(bf16[8,48,1280]{2,1,0:T(8,128)(2,1)} %reshape.186), calls=%async_computation.3 | async-start | bytes 1966080 | tf_op jit(solution)/shard_map/all_to_all | solution.py:19
  172.6 24.7 %all-to-all-start.3 = ((bf16[16,96,320]{2,1,0:T(8,128)(2,1)}), bf16[16,96,320]{2,1,0:T(8,128)(2,1)}, u32[]{:S(2)}, u32[]{:S(2)}) async-start(bf16[16,96,320]{2,1,0:T(8,128)(2,1)} %bitcast.78), calls=%async_computation.4 | async-start | bytes 2359296 | tf_op jit(solution)/shard_map/all_to_all | solution.py:19
  177.0 16.6 %copy-start.1 = (f32[384,1280]{1,0:T(8,128)S(1)}, f32[384,1280]{1,0:T(8,128)}, u32[]{:S(2)}) copy-start(f32[384,1280]{1,0:T(8,128)} %fusion.8) | copy-start | bytes 5898244
  194.0 1.0 copy-start.3
  197.2 3.0 copy-start.6
  200.3 9.2 %copy-start.4 = (bf16[384,640]{1,0:T(8,128)(2,1)}, bf16[384,640]{1,0:T(8,128)(2,1)S(1)}, u32[]{:S(2)}) copy-start(bf16[384,640]{1,0:T(8,128)(2,1)S(1)} %fusion.10) | copy-start | bytes 1474564
  202.5 31.8 %all-to-all-start.4 = ((bf16[16,40,1280]{2,1,0:T(8,128)(2,1)}), bf16[16,40,1280]{2,1,0:T(8,128)(2,1)}, u32[]{:S(2)}, u32[]{:S(2)}) async-start(bf16[16,40,1280]{2,1,0:T(8,128)(2,1)} %bitcast.84), calls=%async_computation.5 | async-start | bytes 3276800 | tf_op jit(solution)/shard_map/all_to_all | solution.py:19
  209.5 1.9 copy-start.13
  225.3 13.6 %copy-start.7 = (bf16[384,1280]{1,0:T(8,128)(2,1)S(1)}, bf16[384,1280]{1,0:T(8,128)(2,1)}, u32[]{:S(2)}) copy-start(bf16[384,1280]{1,0:T(8,128)(2,1)} %convolution_convert_fusion.5) | copy-start | bytes 2949124
  234.3 40.9 %all-to-all-start.5 = ((bf16[16,114,640]{2,1,0:T(8,128)(2,1)}), bf16[16,114,640]{2,1,0:T(8,128)(2,1)}, u32[]{:S(2)}, u32[]{:S(2)}) async-start(bf16[16,114,640]{2,1,0:T(8,128)(2,1)} %pad_maximum_fusion), calls=%async_computation.6 | async-start | bytes 4915200 | tf_op jit(solution)/shard_map/all_to_all | solution.py:19
  239.7 8.2 %collective-permute-start = (bf16[48,1280]{1,0:T(8,128)(2,1)}, bf16[48,1280]{1,0:T(8,128)(2,1)S(1)}, u32[]{:S(2)}, u32[]{:S(2)}) collective-permute-start(bf16[48,1280]{1,0:T(8,128)(2,1)} %get-tuple-element.72), channel_id=1, source_target_pairs={{0,16},{16,32},{32,48},{48,64},{64,80},{80,96},{96,112},{112,0},{1... | collective-permute-start | bytes 368648 | tf_op jit(solution)/shard_map/ppermute | solution.py:35
  241.1 10.6 %collective-permute-start.1 = (bf16[48,1280]{1,0:T(8,128)(2,1)}, bf16[48,1280]{1,0:T(8,128)(2,1)S(1)}, u32[]{:S(2)}, u32[]{:S(2)}) collective-permute-start(bf16[48,1280]{1,0:T(8,128)(2,1)} %get-tuple-element.78), channel_id=1, source_target_pairs={{0,32},{16,48},{32,64},{48,80},{64,96},{80,112},{96,0},{112,16},{1... | collective-permute-start | bytes 368648 | tf_op jit(solution)/shard_map/ppermute | solution.py:35
  242.3 15.0 %collective-permute-start.2 = (bf16[48,1280]{1,0:T(8,128)(2,1)S(1)}, bf16[48,1280]{1,0:T(8,128)(2,1)S(1)}, u32[]{:S(2)}, u32[]{:S(2)}) collective-permute-start(bf16[48,1280]{1,0:T(8,128)(2,1)S(1)} %get-tuple-element.77), channel_id=1, source_target_pairs={{0,48},{16,64},{32,80},{48,96},{64,112},{80,0},{96,16},{112,32},{1... | collective-permute-start | bytes 368648 | tf_op jit(solution)/shard_map/ppermute | solution.py:35
  243.7 13.5 %collective-permute-start.3 = (bf16[48,1280]{1,0:T(8,128)(2,1)S(1)}, bf16[48,1280]{1,0:T(8,128)(2,1)S(1)}, u32[]{:S(2)}, u32[]{:S(2)}) collective-permute-start(bf16[48,1280]{1,0:T(8,128)(2,1)S(1)} %get-tuple-element.76), channel_id=1, source_target_pairs={{0,64},{16,80},{32,96},{48,112},{64,0},{80,16},{96,32},{112,48},{1... | collective-permute-start | bytes 368648 | tf_op jit(solution)/shard_map/ppermute | solution.py:35
  245.2 12.1 %collective-permute-start.4 = (bf16[48,1280]{1,0:T(8,128)(2,1)S(1)}, bf16[48,1280]{1,0:T(8,128)(2,1)S(1)}, u32[]{:S(2)}, u32[]{:S(2)}) collective-permute-start(bf16[48,1280]{1,0:T(8,128)(2,1)S(1)} %get-tuple-element.75), channel_id=1, source_target_pairs={{0,80},{16,96},{32,112},{48,0},{64,16},{80,32},{96,48},{112,64},{1... | collective-permute-start | bytes 368648 | tf_op jit(solution)/shard_map/ppermute | solution.py:35
  247.8 9.4 %collective-permute-start.5 = (bf16[48,1280]{1,0:T(8,128)(2,1)S(1)}, bf16[48,1280]{1,0:T(8,128)(2,1)S(1)}, u32[]{:S(2)}, u32[]{:S(2)}) collective-permute-start(bf16[48,1280]{1,0:T(8,128)(2,1)S(1)} %get-tuple-element.74), channel_id=1, source_target_pairs={{0,96},{16,112},{32,0},{48,16},{64,32},{80,48},{96,64},{112,80},{1... | collective-permute-start | bytes 368648 | tf_op jit(solution)/shard_map/ppermute | solution.py:35
  251.7 6.2 %collective-permute-start.6 = (bf16[48,1280]{1,0:T(8,128)(2,1)S(1)}, bf16[48,1280]{1,0:T(8,128)(2,1)S(1)}, u32[]{:S(2)}, u32[]{:S(2)}) collective-permute-start(bf16[48,1280]{1,0:T(8,128)(2,1)S(1)} %get-tuple-element.73), channel_id=1, source_target_pairs={{0,112},{16,0},{32,16},{48,32},{64,48},{80,64},{96,80},{112,96},{1... | collective-permute-start | bytes 368648 | tf_op jit(solution)/shard_map/ppermute | solution.py:35
  276.6 27.2 %copy-start.14 = (bf16[1024,256]{1,0:T(8,128)(2,1)S(1)}, bf16[1024,256]{1,0:T(8,128)(2,1)}, u32[]{:S(2)}) copy-start(bf16[1024,256]{1,0:T(8,128)(2,1)} %hidden_ref.1) | copy-start | bytes 1572868
  283.8 28.6 %copy-start.16 = (bf16[1024,256]{1,0:T(8,128)(2,1)S(1)}, bf16[1024,256]{1,0:T(8,128)(2,1)}, u32[]{:S(2)}) copy-start(bf16[1024,256]{1,0:T(8,128)(2,1)} %get-tuple-element.44) | copy-start | bytes 1572868
  303.8 8.5 %copy-start.12 = (bf16[1024,5120]{1,0:T(8,128)(2,1)S(1)}, bf16[1024,5120]{1,0:T(8,128)(2,1)}, u32[]{:S(2)}) copy-start(bf16[1024,5120]{1,0:T(8,128)(2,1)} %all-gather.4.cloned.1.call-done) | copy-start | bytes 31457284
Sparse Core Ops, SparseCore 0:
  18.0 65.0 reduce-scatter.1
Sparse Core Ops, SparseCore 1:
  47.7 45.1 all-gather.5
  143.5 42.0 all-gather.7
  188.4 115.3 all-gather.3
